TPU v7x, 32 devices: a whole 2x2x4 slice. The times are simulated.
32 devices in a mesh: dom: 8 (over z, y), grp: 4 (over x, core).
Axes of the slice: x: 2, y: 2, z: 4, core: 2. Of those that a mesh axis runs over, the one named last changes fastest.
Arguments:
- element_faces: int32 [4, 1024], P(None, 'dom'), may hold values from 0 to 1023, as said below
- interior_load: bfloat16 [80, 1024], P(None, 'dom'), may hold values from -6 to 6
- inverses: bfloat16 [80, 80, 1024], P('grp', None, 'dom'), may hold values from -0.625 to 0.625
- lift_operator: float32 [80, 240], P('grp'), may hold values from -0.625 to 0.625
- face_area: float32 [4, 1024], P(None, 'dom'), may hold values from 0.3 to 27
- columns: int32 [7, 1024], P(None, 'dom'), may hold values from -1 to 1023, as said below
- blocks: float32 [7, 60, 60, 1024], P(None, 'grp', None, 'dom'), may hold values from -0.00119 to 0.00119
- diagonal: float32 [60, 1024], P('grp', 'dom'), may hold values from 1.02 to 1.3
Outputs:
- solution: float32 [60, 1024], P('grp', 'dom')
- residual: float32 [60, 1024], P('grp', 'dom')
Inputs may be any that keep to these rules, and one draw needn't show every extreme that they name: `element_faces`: every face block of an element is owned by the element's own index of dom or the one before or after it; an index owns the face blocks i * 128 to (i + 1) * 128 - 1. `columns`: slot 0 of a face block row holds the block itself. Every other nonnegative entry is a face block owned by the row's own index of dom or the one before or after it, and within one slot no number appears twice.
All inputs are finite; a program needn't handle non-finite values.
Results may differ from a plain program's by a relative error of at most 0.0003.
Values sent between devices are 32-bit elements; how exact they have to be, the bound alone decides.
No kernel may reach another device: no remote copies, remote signals or barrier semaphores. Data moves between devices by JAX's collectives and lax.ppermute only.
A program may use at most 64 MiB of HBM per device.

v0:
```python
import jax
import jax.numpy as jnp
from jax import lax
from jax.sharding import PartitionSpec as P

ITERS = 8


def padded(cells, sides, width):
    for axis, dim in sides:
        count = lax.axis_size(axis)
        ends = count - 1
        head = lax.slice_in_dim(cells, 0, width, axis=dim)
        tail = lax.slice_in_dim(cells, cells.shape[dim] - width, cells.shape[dim], axis=dim)
        cells = jnp.concatenate(
            [
                lax.ppermute(tail, axis, [(i, (i + 1) % count) for i in range(ends)]),
                cells,
                lax.ppermute(head, axis, [((i + 1) % count, i) for i in range(ends)]),
            ],
            axis=dim,
        )
    return cells


def shifted(block, axis, distance):
    devices = range(lax.axis_size(axis))
    route = [(i - distance, i) for i in devices if i - distance in devices]
    return lax.ppermute(block, axis, route)


def spread(field_rows):
    faces_here = field_rows.shape[1]
    whole = lax.all_gather(field_rows, "grp", axis=0, tiled=True)
    return padded(whole, (("dom", 1),), faces_here)


def deliver(slab):
    faces_here = slab.shape[1] // 3
    from_upper = shifted(slab[:, :faces_here], "dom", -1)
    from_lower = shifted(slab[:, 2 * faces_here :], "dom", 1)
    summed = slab[:, faces_here : 2 * faces_here] + from_upper + from_lower
    return lax.psum_scatter(summed, "grp", scatter_dimension=0, tiled=True)


def to_slab(entries, targets, faces_here):
    return jax.ops.segment_sum(entries, targets.reshape(-1), num_segments=3 * faces_here).T


def operate(field_rows, blocks, local_index, usable, diagonal):
    slab = spread(field_rows)
    picked = jnp.where(usable[None, :, :], slab[:, local_index], jnp.zeros((), jnp.float32))
    forward = jnp.einsum("sijf,jsf->if", blocks, picked, precision=lax.Precision.HIGHEST)
    transposed = jnp.einsum("sijf,if->sjf", blocks, field_rows, precision=lax.Precision.HIGHEST)
    transposed = jnp.where(usable[:, None, :], transposed, jnp.zeros((), jnp.float32))
    slot_count, height, faces_here = transposed.shape
    entries = jnp.transpose(transposed, (0, 2, 1)).reshape(slot_count * faces_here, height)
    return diagonal * field_rows + forward + deliver(to_slab(entries, local_index, faces_here))


def two_products(residual, image):
    return lax.psum((jnp.sum(residual * residual), jnp.sum(residual * image)), ("dom", "grp"))


def on_device(
    element_faces, interior_load, inverses, lift_operator, face_area, columns, blocks, diagonal
):
    domain = lax.axis_index("dom")
    faces_here = diagonal.shape[1]
    full_width = lift_operator.shape[1] // 4
    elements_here = interior_load.shape[1]
    u_rows = jnp.einsum("ije,je->ie", inverses, interior_load, preferred_element_type=jnp.float32)
    lifted = lax.dot_general(
        lift_operator, u_rows, (((0,), (0,)), ((), ())), precision=lax.Precision.HIGHEST
    )
    contrib = -(lifted.reshape(4, full_width, elements_here) * face_area[:, None, :])
    entries = jnp.transpose(contrib, (0, 2, 1)).reshape(4 * elements_here, full_width)
    slot_faces = element_faces - (domain - 1) * faces_here
    right_side = deliver(to_slab(entries, slot_faces, faces_here))
    usable = columns >= 0
    local_index = jnp.where(usable, columns - (domain - 1) * faces_here, faces_here)
    solution = jnp.zeros_like(right_side)
    residual = right_side
    image = operate(residual, blocks, local_index, usable, diagonal)
    norm_now, product_sum = two_products(residual, image)
    alpha = norm_now / product_sum
    direction, along = (residual, image)
    for iteration in range(ITERS):
        solution = solution + alpha * direction
        residual = residual - alpha * along
        if iteration + 1 < ITERS:
            image = operate(residual, blocks, local_index, usable, diagonal)
            norm_next, product_sum = two_products(residual, image)
            ratio = norm_next / norm_now
            alpha = norm_next / (product_sum - ratio * norm_next / alpha)
            direction = residual + ratio * direction
            along = image + ratio * along
            norm_now = norm_next
    return (solution, residual)


def solution(mesh):
    placed = (
        P(None, "dom"),
        P(None, "dom"),
        P("grp", None, "dom"),
        P("grp", None),
        P(None, "dom"),
        P(None, "dom"),
        P(None, "grp", None, "dom"),
        P("grp", "dom"),
    )
    return jax.shard_map(
        on_device,
        mesh=mesh,
        in_specs=placed,
        out_specs=(P("grp", "dom"), P("grp", "dom")),
        check_vma=False,
    )
```

profile of v0, /device:TPU:0, one launch (start us, length us, event | category | flops | bytes accessed | tf_op | source)
XLA Modules:
  0.0 891.2 jit_solution(9413418805491365049)
XLA Ops:
  4.4 2.3 scatter_custom_fusion
  8.1 5.5 collective-permute-start.1
  17.5 11.5 %all-reduce = f32[60,128]{0,1:T(8,128)S(1)} all-reduce(f32[60,128]{0,1:T(8,128)S(1)} %fusion.26), channel_id=2, replica_groups=mesh['dom'=8,'grp'=4] {'grp'}, use_global_device_ids=true, to_apply=%region_1.0.clone | all-reduce | flops 7680 | bytes 61440
  29.7 5.2 all-gather
  37.0 5.6 collective-permute-start.2
  42.7 3.1 multiply_reduce_fusion.14
  47.6 3.7 gather_fusion
  57.8 7.1 scatter_custom_fusion.1
  67.1 4.8 collective-permute-start.5
  75.4 12.2 %all-reduce.1 = f32[60,128]{0,1:T(8,128)} all-reduce(f32[60,128]{0,1:T(8,128)} %fusion.25), channel_id=3, replica_groups=mesh['dom'=8,'grp'=4] {'grp'}, use_global_device_ids=true, to_apply=%region_5.6.clone | all-reduce | flops 7680 | bytes 61440
  90.6 42.4 %all-reduce.16 = (f32[]{:T(128)}, f32[]{:T(128)}) all-reduce(f32[]{:T(128)} %get-tuple-element.47, f32[]{:T(128)} %get-tuple-element.45), channel_id=1, replica_groups=mesh['dom'=8,'grp'=4] {'dom','grp'}, use_global_device_ids=true, to_apply=%region_3.4 | all-reduce | flops 2 | bytes 16 | tf_op jit(solution)/shard_map/psum | solution.py:62
  134.3 6.0 all-gather.1
  143.2 5.1 collective-permute-start.6
  151.1 3.7 gather_fusion.1
  159.3 1.9 copy.384
  161.2 7.1 scatter_custom_fusion.2
  170.6 5.0 collective-permute-start.9
  179.0 11.9 %all-reduce.2 = f32[60,128]{0,1:T(8,128)} all-reduce(f32[60,128]{0,1:T(8,128)} %fusion.24), channel_id=4, replica_groups=mesh['dom'=8,'grp'=4] {'grp'}, use_global_device_ids=true, to_apply=%region_11.12.clone | all-reduce | flops 7680 | bytes 61440
  194.0 43.8 %all-reduce.15 = (f32[]{:T(128)}, f32[]{:T(128)}) all-reduce(f32[]{:T(128)} %get-tuple-element.21, f32[]{:T(128)} %get-tuple-element.20), channel_id=1, replica_groups=mesh['dom'=8,'grp'=4] {'dom','grp'}, use_global_device_ids=true, to_apply=%region_9.10 | all-reduce | flops 2 | bytes 16 | tf_op jit(solution)/shard_map/psum | solution.py:62
  242.4 6.0 all-gather.2
  252.6 4.7 collective-permute-start.10
  260.6 3.7 gather_fusion.2
  270.8 7.1 scatter_custom_fusion.3
  280.1 5.0 collective-permute-start.13
  288.5 11.7 %all-reduce.3 = f32[60,128]{0,1:T(8,128)} all-reduce(f32[60,128]{0,1:T(8,128)} %fusion.23), channel_id=5, replica_groups=mesh['dom'=8,'grp'=4] {'grp'}, use_global_device_ids=true, to_apply=%region_17.18.clone | all-reduce | flops 7680 | bytes 61440
  303.3 42.9 %all-reduce.14 = (f32[]{:T(128)}, f32[]{:T(128)}) all-reduce(f32[]{:T(128)} %get-tuple-element.19, f32[]{:T(128)} %get-tuple-element.18), channel_id=1, replica_groups=mesh['dom'=8,'grp'=4] {'dom','grp'}, use_global_device_ids=true, to_apply=%region_15.16 | all-reduce | flops 2 | bytes 16 | tf_op jit(solution)/shard_map/psum | solution.py:62
  350.2 6.0 all-gather.3
  360.4 4.9 collective-permute-start.14
  368.4 3.7 gather_fusion.3
  376.6 1.9 copy.386
  378.5 7.1 scatter_custom_fusion.4
  387.9 5.0 collective-permute-start.17
  396.3 11.7 %all-reduce.4 = f32[60,128]{0,1:T(8,128)} all-reduce(f32[60,128]{0,1:T(8,128)} %fusion.22), channel_id=6, replica_groups=mesh['dom'=8,'grp'=4] {'grp'}, use_global_device_ids=true, to_apply=%region_23.24.clone | all-reduce | flops 7680 | bytes 61440
  411.1 43.0 %all-reduce.13 = (f32[]{:T(128)}, f32[]{:T(128)}) all-reduce(f32[]{:T(128)} %get-tuple-element.17, f32[]{:T(128)} %get-tuple-element.16), channel_id=1, replica_groups=mesh['dom'=8,'grp'=4] {'dom','grp'}, use_global_device_ids=true, to_apply=%region_21.22 | all-reduce | flops 2 | bytes 16 | tf_op jit(solution)/shard_map/psum | solution.py:62
  458.2 6.0 all-gather.4
  468.4 4.8 collective-permute-start.18
  476.4 3.7 gather_fusion.4
  484.6 1.9 copy.387
  486.5 7.1 scatter_custom_fusion.5
  495.9 5.0 collective-permute-start.21
  504.3 11.7 %all-reduce.5 = f32[60,128]{0,1:T(8,128)} all-reduce(f32[60,128]{0,1:T(8,128)} %fusion.21), channel_id=7, replica_groups=mesh['dom'=8,'grp'=4] {'grp'}, use_global_device_ids=true, to_apply=%region_29.30.clone | all-reduce | flops 7680 | bytes 61440
  519.1 42.8 %all-reduce.12 = (f32[]{:T(128)}, f32[]{:T(128)}) all-reduce(f32[]{:T(128)} %get-tuple-element.15, f32[]{:T(128)} %get-tuple-element.14), channel_id=1, replica_groups=mesh['dom'=8,'grp'=4] {'dom','grp'}, use_global_device_ids=true, to_apply=%region_27.28 | all-reduce | flops 2 | bytes 16 | tf_op jit(solution)/shard_map/psum | solution.py:62
  566.7 6.0 all-gather.5
  576.9 5.0 collective-permute-start.22
  584.9 3.7 gather_fusion.5
  593.1 1.9 copy.388
  595.0 7.1 scatter_custom_fusion.6
  604.4 5.0 collective-permute-start.25
  612.8 11.7 %all-reduce.6 = f32[60,128]{0,1:T(8,128)} all-reduce(f32[60,128]{0,1:T(8,128)} %fusion.20), channel_id=8, replica_groups=mesh['dom'=8,'grp'=4] {'grp'}, use_global_device_ids=true, to_apply=%region_35.36.clone | all-reduce | flops 7680 | bytes 61440
  629.0 43.1 %all-reduce.11 = (f32[]{:T(128)}, f32[]{:T(128)}) all-reduce(f32[]{:T(128)} %get-tuple-element.13, f32[]{:T(128)} %get-tuple-element.12), channel_id=1, replica_groups=mesh['dom'=8,'grp'=4] {'dom','grp'}, use_global_device_ids=true, to_apply=%region_33.34 | all-reduce | flops 2 | bytes 16 | tf_op jit(solution)/shard_map/psum | solution.py:62
  676.0 6.0 all-gather.6
  686.3 4.7 collective-permute-start.26
  694.2 3.7 gather_fusion.6
  704.4 7.1 scatter_custom_fusion.7
  713.7 5.0 collective-permute-start.29
  722.1 11.7 %all-reduce.7 = f32[60,128]{0,1:T(8,128)} all-reduce(f32[60,128]{0,1:T(8,128)} %fusion.19), channel_id=9, replica_groups=mesh['dom'=8,'grp'=4] {'grp'}, use_global_device_ids=true, to_apply=%region_41.42.clone | all-reduce | flops 7680 | bytes 61440
  737.0 42.9 %all-reduce.10 = (f32[]{:T(128)}, f32[]{:T(128)}) all-reduce(f32[]{:T(128)} %get-tuple-element.11, f32[]{:T(128)} %get-tuple-element.10), channel_id=1, replica_groups=mesh['dom'=8,'grp'=4] {'dom','grp'}, use_global_device_ids=true, to_apply=%region_39.40 | all-reduce | flops 2 | bytes 16 | tf_op jit(solution)/shard_map/psum | solution.py:62
  784.4 6.0 all-gather.7
  794.6 4.9 collective-permute-start.30
  802.5 3.7 gather_fusion.7
  812.7 7.1 scatter_custom_fusion.8
  822.0 5.0 collective-permute-start.33
  829.9 10.7 %all-reduce.8 = f32[60,128]{0,1:T(8,128)S(1)} all-reduce(f32[60,128]{0,1:T(8,128)S(1)} %fusion.18), channel_id=10, replica_groups=mesh['dom'=8,'grp'=4] {'grp'}, use_global_device_ids=true, to_apply=%region_47.48.clone | all-reduce | flops 7680 | bytes 61440
  842.1 43.0 %all-reduce.9 = (f32[]{:T(128)}, f32[]{:T(128)}) all-reduce(f32[]{:T(128)} %get-tuple-element.9, f32[]{:T(128)} %get-tuple-element.8), channel_id=1, replica_groups=mesh['dom'=8,'grp'=4] {'dom','grp'}, use_global_device_ids=true, to_apply=%region_45.46 | all-reduce | flops 2 | bytes 16 | tf_op jit(solution)/shard_map/psum | solution.py:62
  (214 shorter events, 178.7 us)
Async XLA Ops:
  0.6 1.9 copy-start
  6.8 10.7 %collective-permute-start = (f32[60,128]{0,1:T(8,128)S(1)}, f32[60,128]{0,1:T(8,128)S(1)}, u32[]{:S(2)}, u32[]{:S(2)}) collective-permute-start(f32[60,128]{0,1:T(8,128)S(1)} %get-tuple-element.65), channel_id=1, source_target_pairs={{4,0},{8,4},{12,8},{16,12},{20,16},{24,20},{28,24},{5,1},{9,5},{13... | collective-permute-start | bytes 92168 | tf_op jit(solution)/shard_map/ppermute | solution.py:29
  8.1 9.4 %collective-permute-start.1 = (f32[60,128]{0,1:T(8,128)S(1)}, f32[60,128]{0,1:T(8,128)S(1)}, u32[]{:S(2)}, u32[]{:S(2)}) collective-permute-start(f32[60,128]{0,1:T(8,128)S(1)} %get-tuple-element.66), channel_id=1, source_target_pairs={{0,4},{4,8},{8,12},{12,16},{16,20},{20,24},{24,28},{1,5},{5,9},{9,... | collective-permute-start | bytes 92168 | tf_op jit(solution)/shard_map/ppermute | solution.py:29
  35.7 10.2 %collective-permute-start.3 = (f32[60,128]{0,1:T(8,128)}, f32[60,128]{0,1:T(8,128)}, u32[]{:S(2)}, u32[]{:S(2)}) collective-permute-start(f32[60,128]{0,1:T(8,128)} %copy.209), channel_id=1, source_target_pairs={{4,0},{8,4},{12,8},{16,12},{20,16},{24,20},{28,24},{5,1},{9,5},{13... | collective-permute-start | bytes 92168 | tf_op jit(solution)/shard_map/ppermute | solution.py:19
  37.0 8.9 collective-permute-start.2
  45.8 26.1 %copy-start.1 = (f32[7,15,60,128]{3,2,1,0:T(8,128)S(1)}, f32[7,15,60,128]{3,2,1,0:T(8,128)}, u32[]{:S(2)}) copy-start(f32[7,15,60,128]{3,2,1,0:T(8,128)} %param.14) | copy-start | bytes 9676804
  53.2 36.7 %copy-start.2 = (f32[15,128]{1,0:T(8,128)S(1)}, f32[15,128]{1,0:T(8,128)}, u32[]{:S(2)}) copy-start(f32[15,128]{1,0:T(8,128)} %param.15) | copy-start | bytes 23044
  65.8 7.4 collective-permute-start.4
  67.1 6.7 collective-permute-start.5
  141.8 8.6 copy-start.3
  141.8 7.7 collective-permute-start.7
  143.2 7.2 collective-permute-start.6
  169.3 7.7 collective-permute-start.8
  170.6 6.9 collective-permute-start.9
  251.2 8.7 copy-start.4
  251.2 7.3 collective-permute-start.11
  252.6 7.3 collective-permute-start.10
  278.8 7.7 collective-permute-start.12
  280.1 6.9 collective-permute-start.13
  350.2 108.0 %copy-start.14 = (f32[15,128]{1,0:T(8,128)}, f32[15,128]{1,0:T(8,128)S(1)}, u32[]{:S(2)}) copy-start(f32[15,128]{1,0:T(8,128)S(1)} %get-tuple-element.43) | copy-start | bytes 23044
  359.0 8.7 copy-start.5
  359.0 7.4 collective-permute-start.15
  360.4 7.3 collective-permute-start.14
  386.6 7.7 collective-permute-start.16
  387.9 6.9 collective-permute-start.17
  411.1 70.9 %copy-start.13 = (f32[15,128]{1,0:T(8,128)}, f32[15,128]{1,0:T(8,128)S(1)}, u32[]{:S(2)}) copy-start(f32[15,128]{1,0:T(8,128)S(1)} %get-tuple-element.41) | copy-start | bytes 23044
  467.0 8.7 copy-start.6
  467.0 7.3 collective-permute-start.19
  468.4 7.3 collective-permute-start.18
  494.6 7.7 collective-permute-start.20
  495.9 6.9 collective-permute-start.21
  566.7 109.4 %copy-start.12 = (f32[15,128]{1,0:T(8,128)}, f32[15,128]{1,0:T(8,128)S(1)}, u32[]{:S(2)}) copy-start(f32[15,128]{1,0:T(8,128)S(1)} %get-tuple-element.40) | copy-start | bytes 23044
  575.5 8.7 copy-start.7
  575.5 7.5 collective-permute-start.23
  576.9 7.3 collective-permute-start.22
  603.1 7.7 collective-permute-start.24
  604.4 6.9 collective-permute-start.25
  628.9 70.9 %copy-start.11 = (f32[15,128]{1,0:T(8,128)}, f32[15,128]{1,0:T(8,128)S(1)}, u32[]{:S(2)}) copy-start(f32[15,128]{1,0:T(8,128)S(1)} %get-tuple-element.38) | copy-start | bytes 23044
  684.8 8.7 copy-start.8
  684.8 7.3 collective-permute-start.27
  686.3 7.3 collective-permute-start.26
  712.4 7.7 collective-permute-start.28
  713.7 6.9 collective-permute-start.29
  736.3 46.8 %copy-start.10 = (f32[15,128]{1,0:T(8,128)}, f32[15,128]{1,0:T(8,128)S(1)}, u32[]{:S(2)}) copy-start(f32[15,128]{1,0:T(8,128)S(1)} %copy.254) | copy-start | bytes 23044
  793.2 8.6 copy-start.9
  793.2 7.5 collective-permute-start.31
  794.6 7.2 collective-permute-start.30
  820.7 8.3 collective-permute-start.32
  822.0 7.0 collective-permute-start.33
where the time goes:
time: 905 us; the launch traced here: 891 us
  blocking collectives  496 us (55%)
  other arithmetic  131 us (14%)
  local copies, waits for them, and re-layouts  112 us (12%)
  starting transfers between devices  108 us (12%)
  between operations  31.8 us (4%)
  waiting for transfers between devices  12.6 us (1%)
    psum x8, blocking collectives, two_products(): lax.psum((jnp.sum(residual * residual), jnp.sum(residual * image)), ('dom...  344 us
    unnamed x9, blocking collectives  105 us
    scatter-add x9, other arithmetic, to_slab(): jax.ops.segment_sum(entries, targets.reshape(-1), num_segments=3 * faces_...  59.5 us
    ppermute x18, starting transfers between devices, shifted(): return lax.ppermute(block, axis, route)  57.2 us
    all_gather x8, blocking collectives, spread(): whole = lax.all_gather(field_rows, 'grp', axis=0, tiled=True)  46.9 us
    gather x16, local copies, waits for them, and re-layouts, operate(): slab[:, local_index]  44.8 us
    ppermute x8, starting transfers between devices, padded(): lax.ppermute(tail, axis, [(i, (i + 1) % count) for i in range(ends)])  39.8 us
    unnamed x65, local copies, waits for them, and re-layouts  37.4 us
  transfers between devices with their start and end apart: 34, of which 14 were waited for; matrix products, arithmetic and copies ran while one was open for 3% of the time, Pallas kernels for 0%

commit v1 on v0

v1 whole, which is shorter than its diff:
```python
import functools

import jax
import jax.numpy as jnp
from jax import lax
from jax.experimental import pallas as pl
from jax.experimental.pallas import tpu as pltpu
from jax.sharding import PartitionSpec as P

ITERS = 8
SUB = 8
ALL = ("dom", "grp")


def up(n, m):
    return (n + m - 1) // m * m


def parts3(x):
    hi = x.astype(jnp.bfloat16)
    rest = x - hi.astype(jnp.float32)
    mid = rest.astype(jnp.bfloat16)
    low = (rest - mid.astype(jnp.float32)).astype(jnp.bfloat16)
    return jnp.concatenate([hi, mid, low], axis=0)


def sum3(y):
    n = y.shape[0] // 3
    return y[:n] + y[n : 2 * n] + y[2 * n :]


def near(step, n_dom):
    return lax.rem(lax.axis_index("dom") + n_dom - 1 + step, n_dom)


def post(out_ref, slab_ref, n_dom, n_grp, width, faces):
    for t in range(3):
        base = near(t, n_dom) * n_grp
        for q in range(n_grp):
            rows = slab_ref[q * width : (q + 1) * width, t * faces : (t + 1) * faces]
            out_ref[base + q, :width, :] = rows


def owned(recv_ref, n_dom, n_grp, width):
    total = None
    for t in range(3):
        base = near(t, n_dom) * n_grp
        for q in range(n_grp):
            piece = recv_ref[base + q, :width, :]
            total = piece if total is None else total + piece
    return total


def rhs_kernel(n_dom, n_grp, width, inv_ref, load_ref, lift_ref, area_ref, hot_ref, out_ref, slab_ref):
    faces = out_ref.shape[2]
    full = width * n_grp
    load = load_ref[...].astype(jnp.float32)
    rows = [
        jnp.sum(inv_ref[i].astype(jnp.float32) * load, axis=0, keepdims=True)
        for i in range(inv_ref.shape[0])
    ]
    u = jnp.concatenate(rows, axis=0)
    lifted = lax.dot_general(
        lift_ref[...], u, (((0,), (0,)), ((), ())),
        precision=lax.Precision.HIGHEST, preferred_element_type=jnp.float32,
    )
    pad = up(full, 16) - full
    total = None
    for k in range(area_ref.shape[0]):
        entry = -lifted[k * full : (k + 1) * full] * area_ref[k : k + 1, :]
        entry = jnp.concatenate([entry, jnp.zeros((pad, entry.shape[1]), jnp.float32)], axis=0)
        e = entry.shape[1]
        part = jnp.dot(parts3(entry), hot_ref[k * e : (k + 1) * e, :], preferred_element_type=jnp.float32)
        total = part if total is None else total + part
    slab_ref[...] = sum3(total)
    post(out_ref, slab_ref, n_dom, n_grp, width, faces)


def apply_kernel(n_dom, n_grp, recv_ref, r_ref, diag_ref, blocks_ref, hot_ref, back_ref, out_ref, near_ref, slab_ref, pick_ref, turn_ref):
    slots, width, full, faces = blocks_ref.shape
    tall = up(full, 16)
    for t in range(3):
        base = near(t, n_dom) * n_grp
        for q in range(n_grp):
            slab_ref[q * width : (q + 1) * width, t * faces : (t + 1) * faces] = recv_ref[base + q, :width, :]
    slab_ref[full:tall, :] = jnp.zeros((tall - full, 3 * faces), jnp.float32)
    pick_ref[...] = sum3(jnp.dot(parts3(slab_ref[...]), hot_ref[...], preferred_element_type=jnp.float32))
    wide = [jnp.broadcast_to(r_ref[a : a + 1, :], (SUB, faces)) for a in range(width)]
    turn_ref[full:tall, :] = jnp.zeros((tall - full, slots * faces), jnp.float32)
    total = [None] * width
    for low in range(0, full, SUB):
        high = min(low + SUB, full)
        acc = [None] * width
        for s in range(slots):
            cols = slice(s * faces, (s + 1) * faces)
            picked = pick_ref[low:high, cols]
            turned = None
            for a in range(width):
                tile = blocks_ref[s, a, low:high, :]
                forward = tile * picked
                backward = tile * wide[a][: high - low]
                acc[a] = forward if acc[a] is None else acc[a] + forward
                turned = backward if turned is None else turned + backward
            turn_ref[low:high, cols] = turned
        for a in range(width):
            line = jnp.sum(acc[a], axis=0, keepdims=True)
            total[a] = line if total[a] is None else total[a] + line
    forward = jnp.concatenate(total, axis=0)
    slab_ref[...] = sum3(jnp.dot(parts3(turn_ref[...]), back_ref[...], preferred_element_type=jnp.float32))
    post(out_ref, slab_ref, n_dom, n_grp, width, faces)
    r = r_ref[...]
    plain = diag_ref[...] * r + forward
    near_ref[...] = plain
    square = jnp.sum(r * r, axis=0, keepdims=True)
    cross = jnp.sum(r * (plain + forward), axis=0, keepdims=True)
    lane = lax.broadcasted_iota(jnp.int32, (1, faces), 1)
    half = faces // 2
    line = jnp.where(lane < half, square + pltpu.roll(square, half, 1), cross + pltpu.roll(cross, half, 1))
    for n in range(n_dom * n_grp):
        out_ref[n, width : width + 1, :] = line


def start_kernel(n_dom, n_grp, recv_ref, out_ref, r_ref):
    width = r_ref.shape[0]
    r = owned(recv_ref, n_dom, n_grp, width)
    r_ref[...] = r
    for n in range(n_dom * n_grp):
        out_ref[n, :width, :] = r


def update_kernel(n_dom, n_grp, first, last, *refs):
    refs = list(refs)
    recv_ref, near_ref, r_ref = refs[:3]
    del refs[:3]
    if not first:
        s_ref, p_ref, x_ref, scal_ref = refs[:4]
        del refs[:4]
    width, faces = r_ref.shape
    lines = jnp.sum(recv_ref[:, width, :], axis=0, keepdims=True)
    lane = lax.broadcasted_iota(jnp.int32, (1, faces), 1)
    low = lane < faces // 2
    norm = jnp.sum(jnp.where(low, lines, 0.0), axis=1, keepdims=True)
    cross = jnp.sum(jnp.where(low, 0.0, lines), axis=1, keepdims=True)
    w = near_ref[...] + owned(recv_ref, n_dom, n_grp, width)
    r = r_ref[...]
    if first:
        alpha = norm / cross
        s, p = w, r
        x = alpha * p
    else:
        beta = norm / scal_ref[0:1, 0:1]
        alpha = norm / (cross - beta * norm / scal_ref[1:2, 0:1])
        s = w + beta * s_ref[...]
        p = r + beta * p_ref[...]
        x = x_ref[...] + alpha * p
    r = r - alpha * s
    if last:
        xo_ref, ro_ref = refs
        xo_ref[...] = x
        ro_ref[...] = r
        return
    out_ref, ro_ref, so_ref, po_ref, xo_ref, scalo_ref = refs
    for n in range(n_dom * n_grp):
        out_ref[n, :width, :] = r
    ro_ref[...] = r
    so_ref[...] = s
    po_ref[...] = p
    xo_ref[...] = x
    scalo_ref[0:1, :] = jnp.broadcast_to(norm, (1, faces))
    scalo_ref[1:2, :] = jnp.broadcast_to(alpha, (1, faces))


def call(kernel, outs, args, scratch=(), name=None):
    vmem = pl.BlockSpec(memory_space=pltpu.VMEM)
    return pl.pallas_call(
        kernel,
        out_shape=outs,
        in_specs=[vmem] * len(args),
        out_specs=jax.tree.map(lambda _: vmem, outs),
        scratch_shapes=list(scratch),
        name=name,
    )(*args)


def on_device(
    element_faces, interior_load, inverses, lift_operator, face_area, columns, blocks, diagonal
):
    n_dom, n_grp = lax.axis_size("dom"), lax.axis_size("grp")
    slots, width, full, faces = blocks.shape
    tall = up(full, 16)
    pieces = jax.ShapeDtypeStruct((n_dom * n_grp, up(width + 1, SUB), faces), jnp.float32)
    field = jax.ShapeDtypeStruct((width, faces), jnp.float32)
    f32 = jnp.float32

    low_face = (lax.axis_index("dom") - 1) * faces
    window = jnp.arange(3 * faces, dtype=jnp.int32)
    here = jnp.where(columns >= 0, columns - low_face, -1).reshape(-1)
    hot = (window[:, None] == here[None, :]).astype(jnp.bfloat16)
    back = (here[:, None] == window[None, :]).astype(jnp.bfloat16)
    owner = (element_faces - low_face).reshape(-1)
    gathered = (owner[:, None] == window[None, :]).astype(jnp.bfloat16)

    def exchange(v):
        return lax.all_to_all(v, ALL, 0, 0)

    slab = pltpu.VMEM((tall, 3 * faces), f32)
    sent = call(
        functools.partial(rhs_kernel, n_dom, n_grp, width),
        pieces,
        (inverses, interior_load, lift_operator, face_area, gathered),
        [slab],
        name="rhs",
    )
    sent, r = call(
        functools.partial(start_kernel, n_dom, n_grp), (pieces, field), (exchange(sent),), name="start"
    )
    state = ()
    for iteration in range(ITERS):
        sent, plain = call(
            functools.partial(apply_kernel, n_dom, n_grp),
            (pieces, field),
            (exchange(sent), r, diagonal, blocks, hot, back),
            [slab, pltpu.VMEM((tall, slots * faces), f32), pltpu.VMEM((tall, slots * faces), f32)],
            name="apply",
        )
        first, last = iteration == 0, iteration + 1 == ITERS
        outs = (field, field) if last else (pieces, field, field, field, field, jax.ShapeDtypeStruct((2, faces), f32))
        got = call(
            functools.partial(update_kernel, n_dom, n_grp, first, last),
            outs,
            (exchange(sent), plain, r) + state,
            name="update",
        )
        if last:
            return got
        sent, r, *state = got
        state = tuple(state)


def solution(mesh):
    placed = (
        P(None, "dom"),
        P(None, "dom"),
        P("grp", None, "dom"),
        P("grp", None),
        P(None, "dom"),
        P(None, "dom"),
        P(None, "grp", None, "dom"),
        P("grp", "dom"),
    )
    return jax.shard_map(
        on_device,
        mesh=mesh,
        in_specs=placed,
        out_specs=(P("grp", "dom"), P("grp", "dom")),
        check_vma=False,
    )
```

time: 905 us -> 297 us (0.33); the launches traced: 891 us -> 296 us
  blocking collectives: 496 us -> 226 us
  other arithmetic: 131 us -> 3.65 us
  local copies, waits for them, and re-layouts: 112 us -> 0.69 us
  starting transfers between devices: 108 us -> 2.58 us
  Pallas kernels: 0 us -> 54 us
  between operations: 31.8 us -> 0.68 us
    psum x8 -> x0, blocking collectives: 344 us -> none  [two_products(): lax.psum((jnp.sum(residual * residual), jnp.sum(residual * image)), ('dom...]
    all_to_all x0 -> x16, blocking collectives: none -> 226 us  [exchange(): return lax.all_to_all(v, ALL, 0, 0)]
    ppermute x34 -> x0, starting transfers between devices: 108 us -> none  [the longest x18 57.2 us: shifted(): return lax.ppermute(block, axis, route)]
    unnamed x9 -> x0, blocking collectives: 105 us -> none
    scatter-add x9 -> x0, other arithmetic: 59.5 us -> none  [to_slab(): jax.ops.segment_sum(entries, targets.reshape(-1), num_segments=3 * faces_...]
    pallas_call x0 -> x18, Pallas kernels: none -> 54 us  [call(): pl.pallas_call(kernel, out_shape=outs, in_specs=[vmem] * len(args), out_s...]
    all_gather x8 -> x0, blocking collectives: 46.9 us -> none  [spread(): whole = lax.all_gather(field_rows, 'grp', axis=0, tiled=True)]
    gather x16 -> x0, local copies, waits for them, and re-layouts: 44.8 us -> none  [operate(): slab[:, local_index]]
  transfers between devices with their start and end apart: 34 -> 1, of which waited for: 14 -> 1; matrix products, arithmetic and copies ran while one was open for 3% -> 1% of each run, Pallas kernels for 0% -> 0%
where the time goes in v1:
time: 297 us; the launch traced here: 296 us
  blocking collectives  226 us (76%)
  Pallas kernels  54 us (18%)
  waiting for transfers between devices  8.47 us (3%)
  other arithmetic  3.65 us (1%)
    all_to_all x16, blocking collectives, exchange(): return lax.all_to_all(v, ALL, 0, 0)  226 us
    pallas_call x18, Pallas kernels, call(): pl.pallas_call(kernel, out_shape=outs, in_specs=[vmem] * len(args), out_s...  54 us
    all_to_all x1, waiting for transfers between devices, exchange(): return lax.all_to_all(v, ALL, 0, 0)  8.47 us
  transfers between devices with their start and end apart: 1, of which 1 were waited for; matrix products, arithmetic and copies ran while one was open for 1% of the time, Pallas kernels for 0%

profile of v1, /device:TPU:0, one launch (start us, length us, event | category | flops | bytes accessed | tf_op | source)
XLA Modules:
  0.0 295.9 jit_solution(17321235867005080656)
XLA Ops:
  0.6 0.7 subtract_bitcast_fusion
  1.3 0.0 copy-start.1
  1.3 0.9 fusion.2.hot_ref
  2.2 2.7 rhs.1
  4.9 18.0 %all_to_all.85.recv_ref = f32[32,16,128]{2,1,0:T(8,128)} all-to-all(f32[32,16,128]{2,1,0:T(8,128)} %rhs.1), channel_id=1, replica_groups=mesh['dom'=8,'grp'=4] {'dom','grp'}, dimensions={0} | all-to-all | bytes 524288 | tf_op jit(solution)/shard_map/all_to_all | solution.py:204
  22.9 1.7 start.1
  24.5 2.6 all-to-all-start.1
  27.1 0.0 copy-done.1
  27.2 1.1 fusion.1.back_ref
  28.2 1.0 fusion.hot_ref
  29.2 8.5 %all-to-all-done.1.recv_ref = f32[32,16,128]{2,1,0:T(8,128)S(1)} async-done(((f32[32,16,128]{2,1,0:T(8,128)}), f32[32,16,128]{2,1,0:T(8,128)S(1)}, u32[]{:S(2)}, u32[]{:S(2)}) %all-to-all-start.1) | async-done | bytes 262176 | tf_op jit(solution)/shard_map/all_to_all | solution.py:204
  37.7 0.0 copy-start
  37.7 0.7 copy-done
  38.4 4.4 %apply.8 = (f32[32,16,128]{2,1,0:T(8,128)}, f32[15,128]{1,0:T(8,128)}) custom-call(f32[32,16,128]{2,1,0:T(8,128)} %copy-done, f32[15,128]{1,0:T(8,128)} %get-tuple-element.63.r_ref.refs_2_, f32[15,128]{1,0:T(8,128)} %diag_ref.15, f32[7,15,60,128]{3,2,1,0:T(8,128)} %blocks_ref.15, bf16[384,896]{1,0:T(8,128)(2,1)} %fusion.hot_ref, bf16[896,384]{1,0:T(8,128)(2,1)} %fusion.1.back_ref), custom_call_target="tpu_custom_call" | custom-call | tf_op jit(solution)/shard_map/apply/pallas_call | solution.py:175
  42.8 13.9 %all_to_all.86.refs_0_ = f32[32,16,128]{2,1,0:T(8,128)} all-to-all(f32[32,16,128]{2,1,0:T(8,128)} %get-tuple-element.64), channel_id=1, replica_groups=mesh['dom'=8,'grp'=4] {'dom','grp'}, dimensions={0} | all-to-all | bytes 524288 | tf_op jit(solution)/shard_map/all_to_all | solution.py:204
  56.6 1.8 update.8
  58.4 13.9 %all_to_all.87.recv_ref = f32[32,16,128]{2,1,0:T(8,128)} all-to-all(f32[32,16,128]{2,1,0:T(8,128)} %get-tuple-element.66), channel_id=1, replica_groups=mesh['dom'=8,'grp'=4] {'dom','grp'}, dimensions={0} | all-to-all | bytes 524288 | tf_op jit(solution)/shard_map/all_to_all | solution.py:204
  72.3 4.4 %apply.9 = (f32[32,16,128]{2,1,0:T(8,128)}, f32[15,128]{1,0:T(8,128)}) custom-call(f32[32,16,128]{2,1,0:T(8,128)} %all_to_all.87.recv_ref, f32[15,128]{1,0:T(8,128)} %get-tuple-element.67.r_ref.refs_2_, f32[15,128]{1,0:T(8,128)} %diag_ref.15, f32[7,15,60,128]{3,2,1,0:T(8,128)} %blocks_ref.15, bf16[384,896]{1,0:T(8,128)(2,1)} %fusion.hot_ref, ...), custom_call_target="tpu_custom_call" | custom-call | tf_op jit(solution)/shard_map/apply/pallas_call | solution.py:175
  76.6 13.9 %all_to_all.88.refs_0_ = f32[32,16,128]{2,1,0:T(8,128)} all-to-all(f32[32,16,128]{2,1,0:T(8,128)} %get-tuple-element.68), channel_id=1, replica_groups=mesh['dom'=8,'grp'=4] {'dom','grp'}, dimensions={0} | all-to-all | bytes 524288 | tf_op jit(solution)/shard_map/all_to_all | solution.py:204
  90.5 1.9 update.9
  92.4 13.9 %all_to_all.89.recv_ref = f32[32,16,128]{2,1,0:T(8,128)} all-to-all(f32[32,16,128]{2,1,0:T(8,128)} %get-tuple-element.74), channel_id=1, replica_groups=mesh['dom'=8,'grp'=4] {'dom','grp'}, dimensions={0} | all-to-all | bytes 524288 | tf_op jit(solution)/shard_map/all_to_all | solution.py:204
  106.2 4.4 %apply.10 = (f32[32,16,128]{2,1,0:T(8,128)}, f32[15,128]{1,0:T(8,128)}) custom-call(f32[32,16,128]{2,1,0:T(8,128)} %all_to_all.89.recv_ref, f32[15,128]{1,0:T(8,128)} %get-tuple-element.75.r_ref.refs_2_, f32[15,128]{1,0:T(8,128)} %diag_ref.15, f32[7,15,60,128]{3,2,1,0:T(8,128)} %blocks_ref.15, bf16[384,896]{1,0:T(8,128)(2,1)} %fusion.hot_ref, ...), custom_call_target="tpu_custom_call" | custom-call | tf_op jit(solution)/shard_map/apply/pallas_call | solution.py:175
  110.6 13.9 %all_to_all.90.refs_0_ = f32[32,16,128]{2,1,0:T(8,128)} all-to-all(f32[32,16,128]{2,1,0:T(8,128)} %get-tuple-element.76), channel_id=1, replica_groups=mesh['dom'=8,'grp'=4] {'dom','grp'}, dimensions={0} | all-to-all | bytes 524288 | tf_op jit(solution)/shard_map/all_to_all | solution.py:204
  124.4 1.9 update.10
  126.3 13.9 %all_to_all.91.recv_ref = f32[32,16,128]{2,1,0:T(8,128)} all-to-all(f32[32,16,128]{2,1,0:T(8,128)} %get-tuple-element.82), channel_id=1, replica_groups=mesh['dom'=8,'grp'=4] {'dom','grp'}, dimensions={0} | all-to-all | bytes 524288 | tf_op jit(solution)/shard_map/all_to_all | solution.py:204
  140.2 4.4 %apply.11 = (f32[32,16,128]{2,1,0:T(8,128)}, f32[15,128]{1,0:T(8,128)}) custom-call(f32[32,16,128]{2,1,0:T(8,128)} %all_to_all.91.recv_ref, f32[15,128]{1,0:T(8,128)} %get-tuple-element.83.r_ref.refs_2_, f32[15,128]{1,0:T(8,128)} %diag_ref.15, f32[7,15,60,128]{3,2,1,0:T(8,128)} %blocks_ref.15, bf16[384,896]{1,0:T(8,128)(2,1)} %fusion.hot_ref, ...), custom_call_target="tpu_custom_call" | custom-call | tf_op jit(solution)/shard_map/apply/pallas_call | solution.py:175
  144.5 13.9 %all_to_all.92.refs_0_ = f32[32,16,128]{2,1,0:T(8,128)} all-to-all(f32[32,16,128]{2,1,0:T(8,128)} %get-tuple-element.84), channel_id=1, replica_groups=mesh['dom'=8,'grp'=4] {'dom','grp'}, dimensions={0} | all-to-all | bytes 524288 | tf_op jit(solution)/shard_map/all_to_all | solution.py:204
  158.4 1.9 update.11
  160.3 13.9 %all_to_all.93.recv_ref = f32[32,16,128]{2,1,0:T(8,128)} all-to-all(f32[32,16,128]{2,1,0:T(8,128)} %get-tuple-element.90), channel_id=1, replica_groups=mesh['dom'=8,'grp'=4] {'dom','grp'}, dimensions={0} | all-to-all | bytes 524288 | tf_op jit(solution)/shard_map/all_to_all | solution.py:204
  174.1 4.4 %apply.12 = (f32[32,16,128]{2,1,0:T(8,128)}, f32[15,128]{1,0:T(8,128)}) custom-call(f32[32,16,128]{2,1,0:T(8,128)} %all_to_all.93.recv_ref, f32[15,128]{1,0:T(8,128)} %get-tuple-element.91.r_ref.refs_2_, f32[15,128]{1,0:T(8,128)} %diag_ref.15, f32[7,15,60,128]{3,2,1,0:T(8,128)} %blocks_ref.15, bf16[384,896]{1,0:T(8,128)(2,1)} %fusion.hot_ref, ...), custom_call_target="tpu_custom_call" | custom-call | tf_op jit(solution)/shard_map/apply/pallas_call | solution.py:175
  178.5 13.9 %all_to_all.94.refs_0_ = f32[32,16,128]{2,1,0:T(8,128)} all-to-all(f32[32,16,128]{2,1,0:T(8,128)} %get-tuple-element.92), channel_id=1, replica_groups=mesh['dom'=8,'grp'=4] {'dom','grp'}, dimensions={0} | all-to-all | bytes 524288 | tf_op jit(solution)/shard_map/all_to_all | solution.py:204
  192.3 1.9 update.12
  194.2 13.9 %all_to_all.95.recv_ref = f32[32,16,128]{2,1,0:T(8,128)} all-to-all(f32[32,16,128]{2,1,0:T(8,128)} %get-tuple-element.98), channel_id=1, replica_groups=mesh['dom'=8,'grp'=4] {'dom','grp'}, dimensions={0} | all-to-all | bytes 524288 | tf_op jit(solution)/shard_map/all_to_all | solution.py:204
  208.1 4.4 %apply.13 = (f32[32,16,128]{2,1,0:T(8,128)}, f32[15,128]{1,0:T(8,128)}) custom-call(f32[32,16,128]{2,1,0:T(8,128)} %all_to_all.95.recv_ref, f32[15,128]{1,0:T(8,128)} %get-tuple-element.99.r_ref.refs_2_, f32[15,128]{1,0:T(8,128)} %diag_ref.15, f32[7,15,60,128]{3,2,1,0:T(8,128)} %blocks_ref.15, bf16[384,896]{1,0:T(8,128)(2,1)} %fusion.hot_ref, ...), custom_call_target="tpu_custom_call" | custom-call | tf_op jit(solution)/shard_map/apply/pallas_call | solution.py:175
  212.4 13.9 %all_to_all.96.refs_0_ = f32[32,16,128]{2,1,0:T(8,128)} all-to-all(f32[32,16,128]{2,1,0:T(8,128)} %get-tuple-element.100), channel_id=1, replica_groups=mesh['dom'=8,'grp'=4] {'dom','grp'}, dimensions={0} | all-to-all | bytes 524288 | tf_op jit(solution)/shard_map/all_to_all | solution.py:204
  226.3 1.9 update.13
  228.1 13.9 %all_to_all.97.recv_ref = f32[32,16,128]{2,1,0:T(8,128)} all-to-all(f32[32,16,128]{2,1,0:T(8,128)} %get-tuple-element.106), channel_id=1, replica_groups=mesh['dom'=8,'grp'=4] {'dom','grp'}, dimensions={0} | all-to-all | bytes 524288 | tf_op jit(solution)/shard_map/all_to_all | solution.py:204
  242.0 4.4 %apply.14 = (f32[32,16,128]{2,1,0:T(8,128)}, f32[15,128]{1,0:T(8,128)}) custom-call(f32[32,16,128]{2,1,0:T(8,128)} %all_to_all.97.recv_ref, f32[15,128]{1,0:T(8,128)} %get-tuple-element.107.r_ref.refs_2_, f32[15,128]{1,0:T(8,128)} %diag_ref.15, f32[7,15,60,128]{3,2,1,0:T(8,128)} %blocks_ref.15, bf16[384,896]{1,0:T(8,128)(2,1)} %fusion.hot_ref, ...), custom_call_target="tpu_custom_call" | custom-call | tf_op jit(solution)/shard_map/apply/pallas_call | solution.py:175
  246.4 13.9 %all_to_all.98.refs_0_ = f32[32,16,128]{2,1,0:T(8,128)} all-to-all(f32[32,16,128]{2,1,0:T(8,128)} %get-tuple-element.108), channel_id=1, replica_groups=mesh['dom'=8,'grp'=4] {'dom','grp'}, dimensions={0} | all-to-all | bytes 524288 | tf_op jit(solution)/shard_map/all_to_all | solution.py:204
  260.2 1.9 update.14
  262.1 13.9 %all_to_all.99.recv_ref = f32[32,16,128]{2,1,0:T(8,128)} all-to-all(f32[32,16,128]{2,1,0:T(8,128)} %get-tuple-element.114), channel_id=1, replica_groups=mesh['dom'=8,'grp'=4] {'dom','grp'}, dimensions={0} | all-to-all | bytes 524288 | tf_op jit(solution)/shard_map/all_to_all | solution.py:204
  276.0 4.4 %apply.15 = (f32[32,16,128]{2,1,0:T(8,128)}, f32[15,128]{1,0:T(8,128)}) custom-call(f32[32,16,128]{2,1,0:T(8,128)} %all_to_all.99.recv_ref, f32[15,128]{1,0:T(8,128)} %get-tuple-element.115.r_ref.refs_2_, f32[15,128]{1,0:T(8,128)} %diag_ref.15, f32[7,15,60,128]{3,2,1,0:T(8,128)} %blocks_ref.15, bf16[384,896]{1,0:T(8,128)(2,1)} %fusion.hot_ref, ...), custom_call_target="tpu_custom_call" | custom-call | tf_op jit(solution)/shard_map/apply/pallas_call | solution.py:175
  280.3 13.9 %all_to_all.100.refs_0_ = f32[32,16,128]{2,1,0:T(8,128)} all-to-all(f32[32,16,128]{2,1,0:T(8,128)} %get-tuple-element.116), channel_id=1, replica_groups=mesh['dom'=8,'grp'=4] {'dom','grp'}, dimensions={0} | all-to-all | bytes 524288 | tf_op jit(solution)/shard_map/all_to_all | solution.py:204
  294.2 1.8 update.15
  (1 shorter events, 0.0 us)
Async XLA Ops:
  1.3 25.8 %copy-start.1 = (s32[7,128]{1,0:T(8,128)S(1)}, s32[7,128]{1,0:T(8,128)}, u32[]{:S(2)}) copy-start(s32[7,128]{1,0:T(8,128)} %param.13) | copy-start | bytes 10756
  24.5 13.2 %all-to-all-start.1 = ((f32[32,16,128]{2,1,0:T(8,128)}), f32[32,16,128]{2,1,0:T(8,128)S(1)}, u32[]{:S(2)}, u32[]{:S(2)}) async-start(f32[32,16,128]{2,1,0:T(8,128)} %get-tuple-element.62), calls=%async_computation.1 | async-start | bytes 524288 | tf_op jit(solution)/shard_map/all_to_all | solution.py:204
  37.7 0.7 copy-start

commit v2 on v1

--- a/solution.py
+++ b/solution.py
@@ -9,6 +9,7 @@
 
 ITERS = 8
 SUB = 8
+VMEM_GRANT = 16 * 1024 * 1024
 ALL = ("dom", "grp")
 
 
@@ -51,9 +52,28 @@
     return total
 
 
-def rhs_kernel(n_dom, n_grp, width, inv_ref, load_ref, lift_ref, area_ref, hot_ref, out_ref, slab_ref):
+def rhs_kernel(n_dom, n_grp, width, cols_ref, owner_ref, inv_ref, load_ref, lift_ref, area_ref, out_ref, hot_ref, back_ref, slab_ref):
     faces = out_ref.shape[2]
     full = width * n_grp
+    slots, sides = cols_ref.shape[0], owner_ref.shape[0]
+    low_face = (lax.axis_index("dom") - 1) * faces
+    cols = cols_ref[...]
+    here = jnp.where(cols >= 0, cols - low_face, -1)
+    place = lax.broadcasted_iota(jnp.int32, (3 * faces, faces), 0)
+    for s in range(slots):
+        hit = place == here[s : s + 1, :]
+        hot_ref[:, s * faces : (s + 1) * faces] = jnp.where(hit, 1.0, 0.0).astype(jnp.bfloat16)
+    lists = jnp.concatenate([here, owner_ref[...] - low_face], axis=0)
+    tall = up(slots + sides, SUB)
+    blank = jnp.full((tall - slots - sides, faces), -1, jnp.int32)
+    flipped = jnp.concatenate([lists, blank], axis=0).astype(jnp.float32).T
+    window = lax.broadcasted_iota(jnp.int32, (faces, 3 * faces), 1).astype(jnp.float32)
+
+    def scatter_of(n):
+        return jnp.where(window == flipped[:, n : n + 1], 1.0, 0.0).astype(jnp.bfloat16)
+
+    for s in range(slots):
+        back_ref[s * faces : (s + 1) * faces, :] = scatter_of(s)
     load = load_ref[...].astype(jnp.float32)
     rows = [
         jnp.sum(inv_ref[i].astype(jnp.float32) * load, axis=0, keepdims=True)
@@ -66,11 +86,10 @@
     )
     pad = up(full, 16) - full
     total = None
-    for k in range(area_ref.shape[0]):
+    for k in range(sides):
         entry = -lifted[k * full : (k + 1) * full] * area_ref[k : k + 1, :]
         entry = jnp.concatenate([entry, jnp.zeros((pad, entry.shape[1]), jnp.float32)], axis=0)
-        e = entry.shape[1]
-        part = jnp.dot(parts3(entry), hot_ref[k * e : (k + 1) * e, :], preferred_element_type=jnp.float32)
+        part = jnp.dot(parts3(entry), scatter_of(slots + k), preferred_element_type=jnp.float32)
         total = part if total is None else total + part
     slab_ref[...] = sum3(total)
     post(out_ref, slab_ref, n_dom, n_grp, width, faces)
@@ -179,6 +198,7 @@
         out_specs=jax.tree.map(lambda _: vmem, outs),
         scratch_shapes=list(scratch),
         name=name,
+        compiler_params=pltpu.CompilerParams(vmem_limit_bytes=VMEM_GRANT),
     )(*args)
 
 
@@ -192,22 +212,18 @@
     field = jax.ShapeDtypeStruct((width, faces), jnp.float32)
     f32 = jnp.float32
 
-    low_face = (lax.axis_index("dom") - 1) * faces
-    window = jnp.arange(3 * faces, dtype=jnp.int32)
-    here = jnp.where(columns >= 0, columns - low_face, -1).reshape(-1)
-    hot = (window[:, None] == here[None, :]).astype(jnp.bfloat16)
-    back = (here[:, None] == window[None, :]).astype(jnp.bfloat16)
-    owner = (element_faces - low_face).reshape(-1)
-    gathered = (owner[:, None] == window[None, :]).astype(jnp.bfloat16)
-
     def exchange(v):
         return lax.all_to_all(v, ALL, 0, 0)
 
     slab = pltpu.VMEM((tall, 3 * faces), f32)
-    sent = call(
+    sent, hot, back = call(
         functools.partial(rhs_kernel, n_dom, n_grp, width),
-        pieces,
-        (inverses, interior_load, lift_operator, face_area, gathered),
+        (
+            pieces,
+            jax.ShapeDtypeStruct((3 * faces, slots * faces), jnp.bfloat16),
+            jax.ShapeDtypeStruct((slots * faces, 3 * faces), jnp.bfloat16),
+        ),
+        (columns, element_faces, inverses, interior_load, lift_operator, face_area),
         [slab],
         name="rhs",
     )

time: 297 us -> 244 us (0.82)
  Pallas kernels: 54 us -> 13.1 us
  waiting for transfers between devices: 8.47 us -> 0 us
  local copies, waits for them, and re-layouts: 0.69 us -> 7.18 us
  blocking collectives: 226 us -> 222 us
  other arithmetic: 3.65 us -> 0 us
    pallas_call x18, Pallas kernels: 54 us -> 13.1 us  [call(): pl.pallas_call(kernel, out_shape=outs, in_specs=[vmem] * len(args), out_s...]
    all_to_all x1 -> x0, waiting for transfers between devices: 8.47 us -> none  [exchange(): return lax.all_to_all(v, ALL, 0, 0)]
    unnamed x4 -> x18, local copies, waits for them, and re-layouts: 0.69 us -> 7.18 us
    all_to_all x16 -> x17, blocking collectives: 226 us -> 222 us  [exchange(): return lax.all_to_all(v, ALL, 0, 0)]
  transfers between devices with their start and end apart: 1 -> 0, of which waited for: 1 -> 0; matrix products, arithmetic and copies ran while one was open for 1% -> 0% of each run, Pallas kernels for 0% -> 0%
where the time goes in v2:
time: 244 us; the launch traced here: 243 us
  blocking collectives  222 us (91%)
  Pallas kernels  13.1 us (5%)
  local copies, waits for them, and re-layouts  7.18 us (3%)
    all_to_all x17, blocking collectives, exchange(): return lax.all_to_all(v, ALL, 0, 0)  222 us
    pallas_call x18, Pallas kernels, call(): pl.pallas_call(kernel, out_shape=outs, in_specs=[vmem] * len(args), out_s...  13.1 us
    unnamed x18, local copies, waits for them, and re-layouts  7.18 us

profile of v2, /device:TPU:0, one launch (start us, length us, event | category | flops | bytes accessed | tf_op | source)
XLA Modules:
  0.0 243.2 jit_solution(14944319138443202830)
XLA Ops:
  0.6 0.0 copy-start.3
  0.6 1.0 copy-done.3
  1.6 0.0 copy-start.4
  1.6 0.7 copy-done.4
  2.4 0.0 copy-start.5
  2.4 0.7 copy-done.5
  3.1 0.0 copy-start.6
  3.1 0.7 copy-done.6
  3.8 0.0 copy-start.7
  3.8 0.7 copy-done.7
  4.5 0.0 copy-start.8
  4.5 0.7 copy-done.8
  5.2 1.1 rhs.1
  6.2 17.7 %all_to_all.85.recv_ref = f32[32,16,128]{2,1,0:T(8,128)S(1)} all-to-all(f32[32,16,128]{2,1,0:T(8,128)S(1)} %get-tuple-element.65), channel_id=1, replica_groups=mesh['dom'=8,'grp'=4] {'dom','grp'}, dimensions={0} | all-to-all | bytes 524288 | tf_op jit(solution)/shard_map/all_to_all | solution.py:216
  24.0 12.8 %all_to_all.86.recv_ref = f32[32,16,128]{2,1,0:T(8,128)S(1)} all-to-all(f32[32,16,128]{2,1,0:T(8,128)S(1)} %get-tuple-element.66), channel_id=1, replica_groups=mesh['dom'=8,'grp'=4] {'dom','grp'}, dimensions={0} | all-to-all | bytes 524288 | tf_op jit(solution)/shard_map/all_to_all | solution.py:216
  36.7 0.0 copy-start
  36.7 2.0 copy-done
  38.7 0.0 copy-start.2
  38.7 0.7 copy-done.2
  39.4 0.0 copy-start.1
  39.4 1.3 apply.8
  40.7 12.8 %all_to_all.87.refs_0_ = f32[32,16,128]{2,1,0:T(8,128)S(1)} all-to-all(f32[32,16,128]{2,1,0:T(8,128)S(1)} %get-tuple-element.70), channel_id=1, replica_groups=mesh['dom'=8,'grp'=4] {'dom','grp'}, dimensions={0} | all-to-all | bytes 524288 | tf_op jit(solution)/shard_map/all_to_all | solution.py:216
  53.5 0.1 update.8
  53.6 12.8 %all_to_all.88.recv_ref = f32[32,16,128]{2,1,0:T(8,128)S(1)} all-to-all(f32[32,16,128]{2,1,0:T(8,128)S(1)} %get-tuple-element.72), channel_id=1, replica_groups=mesh['dom'=8,'grp'=4] {'dom','grp'}, dimensions={0} | all-to-all | bytes 524288 | tf_op jit(solution)/shard_map/all_to_all | solution.py:216
  66.4 0.0 copy-done.1
  66.4 1.3 apply.9
  67.6 12.8 %all_to_all.89.refs_0_ = f32[32,16,128]{2,1,0:T(8,128)S(1)} all-to-all(f32[32,16,128]{2,1,0:T(8,128)S(1)} %get-tuple-element.74), channel_id=1, replica_groups=mesh['dom'=8,'grp'=4] {'dom','grp'}, dimensions={0} | all-to-all | bytes 524288 | tf_op jit(solution)/shard_map/all_to_all | solution.py:216
  80.4 0.2 update.9
  80.6 12.8 %all_to_all.90.recv_ref = f32[32,16,128]{2,1,0:T(8,128)S(1)} all-to-all(f32[32,16,128]{2,1,0:T(8,128)S(1)} %get-tuple-element.80), channel_id=1, replica_groups=mesh['dom'=8,'grp'=4] {'dom','grp'}, dimensions={0} | all-to-all | bytes 524288 | tf_op jit(solution)/shard_map/all_to_all | solution.py:216
  93.4 1.3 apply.10
  94.6 12.8 %all_to_all.91.refs_0_ = f32[32,16,128]{2,1,0:T(8,128)S(1)} all-to-all(f32[32,16,128]{2,1,0:T(8,128)S(1)} %get-tuple-element.82), channel_id=1, replica_groups=mesh['dom'=8,'grp'=4] {'dom','grp'}, dimensions={0} | all-to-all | bytes 524288 | tf_op jit(solution)/shard_map/all_to_all | solution.py:216
  107.4 0.2 update.10
  107.6 12.8 %all_to_all.92.recv_ref = f32[32,16,128]{2,1,0:T(8,128)S(1)} all-to-all(f32[32,16,128]{2,1,0:T(8,128)S(1)} %get-tuple-element.88), channel_id=1, replica_groups=mesh['dom'=8,'grp'=4] {'dom','grp'}, dimensions={0} | all-to-all | bytes 524288 | tf_op jit(solution)/shard_map/all_to_all | solution.py:216
  120.4 1.2 apply.11
  121.6 12.8 %all_to_all.93.refs_0_ = f32[32,16,128]{2,1,0:T(8,128)S(1)} all-to-all(f32[32,16,128]{2,1,0:T(8,128)S(1)} %get-tuple-element.90), channel_id=1, replica_groups=mesh['dom'=8,'grp'=4] {'dom','grp'}, dimensions={0} | all-to-all | bytes 524288 | tf_op jit(solution)/shard_map/all_to_all | solution.py:216
  134.4 0.2 update.11
  134.6 12.8 %all_to_all.94.recv_ref = f32[32,16,128]{2,1,0:T(8,128)S(1)} all-to-all(f32[32,16,128]{2,1,0:T(8,128)S(1)} %get-tuple-element.96), channel_id=1, replica_groups=mesh['dom'=8,'grp'=4] {'dom','grp'}, dimensions={0} | all-to-all | bytes 524288 | tf_op jit(solution)/shard_map/all_to_all | solution.py:216
  147.4 1.3 apply.12
  148.6 12.8 %all_to_all.95.refs_0_ = f32[32,16,128]{2,1,0:T(8,128)S(1)} all-to-all(f32[32,16,128]{2,1,0:T(8,128)S(1)} %get-tuple-element.98), channel_id=1, replica_groups=mesh['dom'=8,'grp'=4] {'dom','grp'}, dimensions={0} | all-to-all | bytes 524288 | tf_op jit(solution)/shard_map/all_to_all | solution.py:216
  161.4 0.2 update.12
  161.6 12.8 %all_to_all.96.recv_ref = f32[32,16,128]{2,1,0:T(8,128)S(1)} all-to-all(f32[32,16,128]{2,1,0:T(8,128)S(1)} %get-tuple-element.104), channel_id=1, replica_groups=mesh['dom'=8,'grp'=4] {'dom','grp'}, dimensions={0} | all-to-all | bytes 524288 | tf_op jit(solution)/shard_map/all_to_all | solution.py:216
  174.4 1.2 apply.13
  175.6 12.8 %all_to_all.97.refs_0_ = f32[32,16,128]{2,1,0:T(8,128)S(1)} all-to-all(f32[32,16,128]{2,1,0:T(8,128)S(1)} %get-tuple-element.106), channel_id=1, replica_groups=mesh['dom'=8,'grp'=4] {'dom','grp'}, dimensions={0} | all-to-all | bytes 524288 | tf_op jit(solution)/shard_map/all_to_all | solution.py:216
  188.4 0.2 update.13
  188.6 12.8 %all_to_all.98.recv_ref = f32[32,16,128]{2,1,0:T(8,128)S(1)} all-to-all(f32[32,16,128]{2,1,0:T(8,128)S(1)} %get-tuple-element.112), channel_id=1, replica_groups=mesh['dom'=8,'grp'=4] {'dom','grp'}, dimensions={0} | all-to-all | bytes 524288 | tf_op jit(solution)/shard_map/all_to_all | solution.py:216
  201.3 1.3 apply.14
  202.6 12.8 %all_to_all.99.refs_0_ = f32[32,16,128]{2,1,0:T(8,128)S(1)} all-to-all(f32[32,16,128]{2,1,0:T(8,128)S(1)} %get-tuple-element.114), channel_id=1, replica_groups=mesh['dom'=8,'grp'=4] {'dom','grp'}, dimensions={0} | all-to-all | bytes 524288 | tf_op jit(solution)/shard_map/all_to_all | solution.py:216
  215.4 0.2 update.14
  215.6 12.8 %all_to_all.100.recv_ref = f32[32,16,128]{2,1,0:T(8,128)S(1)} all-to-all(f32[32,16,128]{2,1,0:T(8,128)S(1)} %get-tuple-element.120), channel_id=1, replica_groups=mesh['dom'=8,'grp'=4] {'dom','grp'}, dimensions={0} | all-to-all | bytes 524288 | tf_op jit(solution)/shard_map/all_to_all | solution.py:216
  228.4 1.3 apply.15
  229.6 12.8 %all_to_all.101.refs_0_ = f32[32,16,128]{2,1,0:T(8,128)S(1)} all-to-all(f32[32,16,128]{2,1,0:T(8,128)S(1)} %get-tuple-element.122), channel_id=1, replica_groups=mesh['dom'=8,'grp'=4] {'dom','grp'}, dimensions={0} | all-to-all | bytes 524288 | tf_op jit(solution)/shard_map/all_to_all | solution.py:216
  242.4 0.7 update.15
  (1 shorter events, 0.0 us)
Async XLA Ops:
  0.6 1.0 copy-start.3
  1.6 0.7 copy-start.4
  2.4 0.7 copy-start.5
  3.1 0.7 copy-start.6
  3.8 0.7 copy-start.7
  4.5 0.7 copy-start.8
  36.7 2.0 copy-start
  38.7 0.7 copy-start.2
  39.4 26.9 %copy-start.1 = (f32[7,15,60,128]{3,2,1,0:T(8,128)S(1)}, f32[7,15,60,128]{3,2,1,0:T(8,128)}, u32[]{:S(2)}) copy-start(f32[7,15,60,128]{3,2,1,0:T(8,128)} %blocks_ref.15) | copy-start | bytes 9676804

commit v3 on v2

v3 whole, which is shorter than its diff:
```python
import functools

import jax
import jax.numpy as jnp
from jax import lax
from jax.experimental import pallas as pl
from jax.experimental.pallas import tpu as pltpu
from jax.sharding import PartitionSpec as P

ITERS = 8
SUB = 8
ALL = ("dom", "grp")
VMEM_GRANT = 16 * 1024 * 1024


def up(n, m):
    return (n + m - 1) // m * m


def parts3(x):
    hi = x.astype(jnp.bfloat16)
    rest = x - hi.astype(jnp.float32)
    mid = rest.astype(jnp.bfloat16)
    low = (rest - mid.astype(jnp.float32)).astype(jnp.bfloat16)
    return jnp.concatenate([hi, mid, low], axis=0)


def sum3(y):
    n = y.shape[0] // 3
    return y[:n] + y[n : 2 * n] + y[2 * n :]


class Plan:
    def __init__(self, width, faces):
        self.n_dom, self.n_grp = lax.axis_size("dom"), lax.axis_size("grp")
        self.width, self.faces = width, faces
        self.half = width // 2
        self.rows = self.half + 1
        self.tall = up(self.rows, SUB)

    def base(self, shift, lower):
        shift += self.n_dom // 2 if lower else 0
        return lax.rem(lax.axis_index("dom") + (shift + self.n_dom), self.n_dom) * self.n_grp

    def kept(self, shift):
        return self.base(shift - self.n_dom // 2, False)

    def left(self):
        return lax.broadcasted_iota(jnp.int32, (1, self.faces), 1) < self.faces // 2

    def split(self, rows, line):
        h, left = self.half, self.left()
        middle = rows[h : h + 1]
        upper = jnp.where(left, middle, line)
        lower = jnp.where(left, pltpu.roll(middle, self.faces // 2, 1), line)
        return (
            jnp.concatenate([rows[:h], upper], axis=0),
            jnp.concatenate([rows[h + 1 :], lower], axis=0),
        )

    def join(self, upper, lower):
        h = self.half
        middle = jnp.where(self.left(), upper[h : h + 1], pltpu.roll(lower[h : h + 1], self.faces // 2, 1))
        return jnp.concatenate([upper[:h], middle, lower[:h]], axis=0)

    def post(self, out_ref, slab_ref, line):
        w, f = self.width, self.faces
        for t in range(3):
            for q in range(self.n_grp):
                rows = slab_ref[q * w : (q + 1) * w, t * f : (t + 1) * f]
                for lower, piece in enumerate(self.split(rows, line)):
                    out_ref[self.base(t - 1, lower) + q, : self.rows, :] = piece

    def owned(self, recv_ref):
        sums = []
        for first in (functools.partial(self.base, lower=False), self.kept):
            total = None
            for t in range(3):
                for q in range(self.n_grp):
                    piece = recv_ref[first(t - 1) + q, : self.rows, :]
                    total = piece if total is None else total + piece
            row = lax.broadcasted_iota(jnp.int32, (self.rows, self.faces), 0)
            lane = lax.broadcasted_iota(jnp.int32, (self.rows, self.faces), 1)
            sums.append(jnp.where((row < self.half) | (lane < self.faces // 2), total, 0.0))
        return sums

    def spread(self, out_ref, halves):
        for first, piece in zip((functools.partial(self.base, lower=False), self.kept), halves):
            for t in range(3):
                for q in range(self.n_grp):
                    out_ref[first(t - 1) + q, : self.rows, :] = piece


def rhs_kernel(width, cols_hbm, owner_hbm, inv_hbm, load_hbm, lift_hbm, area_hbm, diag_hbm, blocks_hbm, out_ref, hot_ref, back_ref, diag_ref, blocks_ref, cols_ref, owner_ref, inv_ref, load_ref, lift_ref, area_ref, slab_ref, sems):
    fetches = [
        pltpu.make_async_copy(src, dst, sems.at[n])
        for n, (src, dst) in enumerate(
            (
                (cols_hbm, cols_ref), (owner_hbm, owner_ref), (load_hbm, load_ref), (inv_hbm, inv_ref),
                (lift_hbm, lift_ref), (area_hbm, area_ref), (diag_hbm, diag_ref), (blocks_hbm, blocks_ref),
            )
        )
    ]
    for fetch in fetches:
        fetch.start()
    faces = out_ref.shape[2]
    plan = Plan(width, faces)
    full = width * plan.n_grp
    slots, sides = cols_ref.shape[0], owner_ref.shape[0]
    low_face = (lax.axis_index("dom") - 1) * faces
    for fetch in fetches[:2]:
        fetch.wait()
    cols = cols_ref[...]
    here = jnp.where(cols >= 0, cols - low_face, -1)
    place = lax.broadcasted_iota(jnp.int32, (3 * faces, faces), 0)
    for s in range(slots):
        hit = place == here[s : s + 1, :]
        hot_ref[:, s * faces : (s + 1) * faces] = jnp.where(hit, 1.0, 0.0).astype(jnp.bfloat16)
    lists = jnp.concatenate([here, owner_ref[...] - low_face], axis=0)
    tall = up(slots + sides, SUB)
    blank = jnp.full((tall - slots - sides, faces), -1, jnp.int32)
    flipped = jnp.concatenate([lists, blank], axis=0).astype(jnp.float32).T
    window = lax.broadcasted_iota(jnp.int32, (faces, 3 * faces), 1).astype(jnp.float32)

    def scatter_of(n):
        return jnp.where(window == flipped[:, n : n + 1], 1.0, 0.0).astype(jnp.bfloat16)

    for s in range(slots):
        back_ref[s * faces : (s + 1) * faces, :] = scatter_of(s)
    for fetch in fetches[2:6]:
        fetch.wait()
    load = load_ref[...].astype(jnp.float32)
    rows = [
        jnp.sum(inv_ref[i].astype(jnp.float32) * load, axis=0, keepdims=True)
        for i in range(inv_ref.shape[0])
    ]
    u = jnp.concatenate(rows, axis=0)
    lifted = lax.dot_general(
        lift_ref[...], u, (((0,), (0,)), ((), ())),
        precision=lax.Precision.HIGHEST, preferred_element_type=jnp.float32,
    )
    pad = up(full, 16) - full
    total = None
    for k in range(sides):
        entry = -lifted[k * full : (k + 1) * full] * area_ref[k : k + 1, :]
        entry = jnp.concatenate([entry, jnp.zeros((pad, entry.shape[1]), jnp.float32)], axis=0)
        part = jnp.dot(parts3(entry), scatter_of(slots + k), preferred_element_type=jnp.float32)
        total = part if total is None else total + part
    slab_ref[...] = sum3(total)
    plan.post(out_ref, slab_ref, jnp.zeros((1, faces), jnp.float32))
    for fetch in fetches[6:]:
        fetch.wait()


def start_kernel(width, recv_ref, out_ref, r_ref):
    plan = Plan(width, recv_ref.shape[2])
    halves = plan.owned(recv_ref)
    plan.spread(out_ref, halves)
    r_ref[...] = jnp.stack(halves)


def apply_kernel(last, recv_ref, diag_ref, blocks_ref, hot_ref, back_ref, out_ref, own_ref, slab_ref, pick_ref, turn_ref):
    slots, width, full, faces = blocks_ref.shape
    plan = Plan(width, faces)
    n_dom, n_grp = plan.n_dom, plan.n_grp
    tall = slab_ref.shape[0]
    for t in range(3):
        for q in range(n_grp):
            rows = plan.join(*(recv_ref[plan.base(t - 1, lower) + q, : plan.rows, :] for lower in (False, True)))
            slab_ref[q * width : (q + 1) * width, t * faces : (t + 1) * faces] = rows
    me = lax.axis_index("grp")
    r = plan.join(*(recv_ref[plan.base(0, lower) + me, : plan.rows, :] for lower in (False, True)))
    own_ref[...] = r
    slab_ref[full:tall, :] = jnp.zeros((tall - full, 3 * faces), jnp.float32)
    pick_ref[...] = sum3(jnp.dot(parts3(slab_ref[...]), hot_ref[...], preferred_element_type=jnp.float32))
    wide = [jnp.broadcast_to(r[a : a + 1, :], (SUB, faces)) for a in range(width)]
    turn_ref[full:tall, :] = jnp.zeros((tall - full, slots * faces), jnp.float32)
    total = [None] * width
    for low in range(0, full, SUB):
        high = min(low + SUB, full)
        acc = [None] * width
        for s in range(slots):
            cols = slice(s * faces, (s + 1) * faces)
            picked = pick_ref[low:high, cols]
            turned = None
            for a in range(width):
                tile = blocks_ref[s, a, low:high, :]
                forward = tile * picked
                backward = tile * wide[a][: high - low]
                acc[a] = forward if acc[a] is None else acc[a] + forward
                turned = backward if turned is None else turned + backward
            turn_ref[low:high, cols] = turned
        for a in range(width):
            line = jnp.sum(acc[a], axis=0, keepdims=True)
            total[a] = line if total[a] is None else total[a] + line
    forward = jnp.concatenate(total, axis=0)
    plain = diag_ref[...] * r + forward
    square = jnp.sum(r * r, axis=0, keepdims=True)
    cross = jnp.sum(r * (plain + forward), axis=0, keepdims=True)
    fold = []
    for line in (square, cross):
        line = line + pltpu.roll(line, faces // 2, 1)
        fold.append(line + pltpu.roll(line, faces // 4, 1))
    lane = lax.broadcasted_iota(jnp.int32, (1, faces), 1)
    line = jnp.where(lane < faces // 4 * 3, fold[0], fold[1])
    slab_ref[...] = sum3(jnp.dot(parts3(turn_ref[...]), back_ref[...], preferred_element_type=jnp.float32))
    if last:
        for n in range(n_dom * n_grp):
            out_ref[n, width : width + 1, :] = line
        for t in range(3):
            for q in range(n_grp):
                rows = slab_ref[q * width : (q + 1) * width, t * faces : (t + 1) * faces]
                out_ref[plan.base(t - 1, False) + q, :width, :] = rows
        mine = plan.base(0, False) + me
        out_ref[mine, :width, :] = out_ref[mine, :width, :] + plain
        return
    for n in range(n_dom * n_grp):
        out_ref[n, plan.half : plan.rows, :] = line
    plan.post(out_ref, slab_ref, line)
    for lower, piece in enumerate(plan.split(plain, jnp.zeros((1, faces), jnp.float32))):
        mine = plan.base(0, lower) + me
        out_ref[mine, : plan.rows, :] = out_ref[mine, : plan.rows, :] + piece


def scalars(lines, faces, scal_ref):
    lines = jnp.sum(lines, axis=0, keepdims=True)
    lane = lax.broadcasted_iota(jnp.int32, (1, faces), 1)
    norm_at = (lane >= faces // 2) & (lane < faces // 4 * 3)
    norm = jnp.sum(jnp.where(norm_at, lines, 0.0), axis=1, keepdims=True)
    cross = jnp.sum(jnp.where(lane >= faces // 4 * 3, lines, 0.0), axis=1, keepdims=True)
    if scal_ref is None:
        return norm, norm / cross, None
    beta = norm / scal_ref[0:1, 0:1]
    return norm, norm / (cross - beta * norm / scal_ref[1:2, 0:1]), beta


def update_kernel(first, width, *refs):
    recv_ref, own_ref, r_ref = refs[:3]
    s_ref, p_ref, x_ref, scal_ref = (None,) * 4 if first else refs[3:7]
    out_ref, ro_ref, so_ref, po_ref, xo_ref, scalo_ref = refs[-6:]
    faces = own_ref.shape[1]
    plan = Plan(width, faces)
    norm, alpha, beta = scalars(recv_ref[:, plan.half, :], faces, scal_ref)
    own = own_ref[...]
    p = own if first else own + beta * p_ref[...]
    po_ref[...] = p
    xo_ref[...] = alpha * p if first else x_ref[...] + alpha * p
    halves = []
    for n, w in enumerate(plan.owned(recv_ref)):
        s = w if first else w + beta * s_ref[n]
        so_ref[n] = s
        halves.append(r_ref[n] - alpha * s)
        ro_ref[n] = halves[n]
    plan.spread(out_ref, halves)
    scalo_ref[0:1, :] = jnp.broadcast_to(norm, (1, faces))
    scalo_ref[1:2, :] = jnp.broadcast_to(alpha, (1, faces))


def finish_kernel(width, recv_ref, own_ref, past_ref, p_ref, x_ref, scal_ref, xo_ref, ro_ref):
    faces = own_ref.shape[1]
    plan = Plan(width, faces)
    _, alpha, beta = scalars(recv_ref[:, width, :], faces, scal_ref)
    w = None
    for t in range(3):
        for q in range(plan.n_grp):
            piece = recv_ref[plan.base(t - 1, False) + q, :width, :]
            w = piece if w is None else w + piece
    own = own_ref[...]
    before = (past_ref[...] - own) / scal_ref[1:2, 0:1]
    xo_ref[...] = x_ref[...] + alpha * (own + beta * p_ref[...])
    ro_ref[...] = own - alpha * (w + beta * before)


def call(kernel, outs, args, scratch=(), name=None, space=pltpu.VMEM):
    vmem = pl.BlockSpec(memory_space=pltpu.VMEM)
    return pl.pallas_call(
        kernel,
        out_shape=outs,
        in_specs=[pl.BlockSpec(memory_space=space)] * len(args),
        out_specs=jax.tree.map(lambda _: vmem, outs),
        scratch_shapes=list(scratch),
        name=name,
        compiler_params=pltpu.CompilerParams(vmem_limit_bytes=VMEM_GRANT),
    )(*args)


def on_device(
    element_faces, interior_load, inverses, lift_operator, face_area, columns, blocks, diagonal
):
    n_dom, n_grp = lax.axis_size("dom"), lax.axis_size("grp")
    slots, width, full, faces = blocks.shape
    if width % 2 == 0 or n_dom < 6:
        raise ValueError("unsupported split")
    tall = up(full, 16)
    f32 = jnp.float32
    plan = Plan(width, faces)
    pieces = jax.ShapeDtypeStruct((n_dom * n_grp, plan.tall, faces), f32)
    wide_pieces = jax.ShapeDtypeStruct((n_dom * n_grp, up(width + 1, SUB), faces), f32)
    field = jax.ShapeDtypeStruct((width, faces), f32)
    halves = jax.ShapeDtypeStruct((2, plan.rows, faces), f32)

    def exchange(v):
        return lax.all_to_all(v, ALL, 0, 0)

    slab = pltpu.VMEM((tall, 3 * faces), f32)
    inputs = (columns, element_faces, inverses, interior_load, lift_operator, face_area)
    sent, hot, back, diag, held = call(
        functools.partial(rhs_kernel, width),
        (
            pieces,
            jax.ShapeDtypeStruct((3 * faces, slots * faces), jnp.bfloat16),
            jax.ShapeDtypeStruct((slots * faces, 3 * faces), jnp.bfloat16),
            field,
            jax.ShapeDtypeStruct(blocks.shape, f32),
        ),
        inputs + (diagonal, blocks),
        [pltpu.VMEM(a.shape, a.dtype) for a in inputs] + [slab, pltpu.SemaphoreType.DMA((len(inputs) + 2,))],
        name="rhs",
        space=pl.ANY,
    )
    sent, r = call(functools.partial(start_kernel, width), (pieces, halves), (exchange(sent),), name="start")
    past, state = None, ()
    for iteration in range(ITERS):
        first, last = iteration == 0, iteration + 1 == ITERS
        sent, own = call(
            functools.partial(apply_kernel, last),
            (wide_pieces if last else pieces, field),
            (exchange(sent), diag, held, hot, back),
            [slab, pltpu.VMEM((tall, slots * faces), f32), pltpu.VMEM((tall, slots * faces), f32)],
            name="apply",
        )
        got = exchange(sent)
        if last:
            _, p, x, scal = state
            return call(
                functools.partial(finish_kernel, width), (field, field), (got, own, past, p, x, scal), name="finish"
            )
        sent, r, *state = call(
            functools.partial(update_kernel, first, width),
            (pieces, halves, halves, field, field, jax.ShapeDtypeStruct((2, faces), f32)),
            (got, own, r) + tuple(state),
            name="update",
        )
        past = own


def solution(mesh):
    placed = (
        P(None, "dom"),
        P(None, "dom"),
        P("grp", None, "dom"),
        P("grp", None),
        P(None, "dom"),
        P(None, "dom"),
        P(None, "grp", None, "dom"),
        P("grp", "dom"),
    )
    return jax.shard_map(
        on_device,
        mesh=mesh,
        in_specs=placed,
        out_specs=(P("grp", "dom"), P("grp", "dom")),
        check_vma=False,
    )
```

time: 244 us -> 202 us (0.83)
  blocking collectives: 222 us -> 177 us
  Pallas kernels: 13.1 us -> 15.7 us
    all_to_all x17, blocking collectives: 222 us -> 177 us  [exchange(): return lax.all_to_all(v, ALL, 0, 0)]
    pallas_call x18, Pallas kernels: 13.1 us -> 15.7 us  [call(): pl.pallas_call(kernel, out_shape=outs, in_specs=[pl.BlockSpec(memory_spac...]
    unnamed x18 -> x16, local copies, waits for them, and re-layouts: 7.18 us -> 7.18 us
where the time goes in v3:
time: 202 us; the launch traced here: 201 us
  blocking collectives  177 us (88%)
  Pallas kernels  15.7 us (8%)
  local copies, waits for them, and re-layouts  7.18 us (4%)
    all_to_all x17, blocking collectives, exchange(): return lax.all_to_all(v, ALL, 0, 0)  177 us
    pallas_call x18, Pallas kernels, call(): pl.pallas_call(kernel, out_shape=outs, in_specs=[pl.BlockSpec(memory_spac...  15.7 us
    unnamed x16, local copies, waits for them, and re-layouts  7.18 us

profile of v3, /device:TPU:0, one launch (start us, length us, event | category | flops | bytes accessed | tf_op | source)
XLA Modules:
  0.0 200.8 jit_solution(2233955609295630695)
XLA Ops:
  0.6 0.0 copy-start
  0.6 2.0 copy-done
  2.6 0.0 copy-start.1
  2.6 1.0 copy-done.1
  3.6 0.0 copy-start.2
  3.6 0.7 copy-done.2
  4.3 0.0 copy-start.3
  4.3 0.7 copy-done.3
  5.1 0.0 copy-start.4
  5.1 0.7 copy-done.4
  5.8 0.0 copy-start.5
  5.8 0.7 copy-done.5
  6.5 0.0 copy-start.6
  6.5 0.7 copy-done.6
  7.1 0.0 copy-start.7
  7.1 0.7 copy-done.7
  7.8 2.2 %rhs.1 = (f32[32,8,128]{2,1,0:T(8,128)S(1)}, bf16[384,896]{1,0:T(8,128)(2,1)S(1)}, bf16[896,384]{1,0:T(8,128)(2,1)S(1)}, f32[15,128]{1,0:T(8,128)S(1)}, f32[7,15,60,128]{3,2,1,0:T(8,128)S(1)}) custom-call(s32[7,128]{1,0:T(8,128)S(1)} %copy-done.5, s32[4,128]{1,0:T(4,128)S(1)} %copy-done.6, bf16[20,80,128]{2,1,0:T(8,128)(2,1)S(1)} %copy-done.1, ...), custom_call_target="tpu_custom_call" | custom-call | tf_op jit(solution)/shard_map/rhs/pallas_call | solution.py:276
  10.0 15.3 %all_to_all.85.recv_ref = f32[32,8,128]{2,1,0:T(8,128)S(1)} all-to-all(f32[32,8,128]{2,1,0:T(8,128)S(1)} %get-tuple-element.65), channel_id=1, replica_groups=mesh['dom'=8,'grp'=4] {'dom','grp'}, dimensions={0} | all-to-all | bytes 262144 | tf_op jit(solution)/shard_map/all_to_all | solution.py:303
  25.4 10.0 %all_to_all.86.recv_ref = f32[32,8,128]{2,1,0:T(8,128)S(1)} all-to-all(f32[32,8,128]{2,1,0:T(8,128)S(1)} %get-tuple-element.66), channel_id=1, replica_groups=mesh['dom'=8,'grp'=4] {'dom','grp'}, dimensions={0} | all-to-all | bytes 262144 | tf_op jit(solution)/shard_map/all_to_all | solution.py:303
  35.4 1.4 apply.8
  36.8 10.0 %all_to_all.87.refs_0_ = f32[32,8,128]{2,1,0:T(8,128)S(1)} all-to-all(f32[32,8,128]{2,1,0:T(8,128)S(1)} %get-tuple-element.71), channel_id=1, replica_groups=mesh['dom'=8,'grp'=4] {'dom','grp'}, dimensions={0} | all-to-all | bytes 262144 | tf_op jit(solution)/shard_map/all_to_all | solution.py:303
  46.7 0.1 update.7
  46.8 10.0 %all_to_all.88.recv_ref = f32[32,8,128]{2,1,0:T(8,128)S(1)} all-to-all(f32[32,8,128]{2,1,0:T(8,128)S(1)} %get-tuple-element.74), channel_id=1, replica_groups=mesh['dom'=8,'grp'=4] {'dom','grp'}, dimensions={0} | all-to-all | bytes 262144 | tf_op jit(solution)/shard_map/all_to_all | solution.py:303
  56.8 1.4 apply.9
  58.2 10.0 %all_to_all.89.refs_0_ = f32[32,8,128]{2,1,0:T(8,128)S(1)} all-to-all(f32[32,8,128]{2,1,0:T(8,128)S(1)} %get-tuple-element.75), channel_id=1, replica_groups=mesh['dom'=8,'grp'=4] {'dom','grp'}, dimensions={0} | all-to-all | bytes 262144 | tf_op jit(solution)/shard_map/all_to_all | solution.py:303
  68.2 0.2 update.8
  68.3 10.0 %all_to_all.90.recv_ref = f32[32,8,128]{2,1,0:T(8,128)S(1)} all-to-all(f32[32,8,128]{2,1,0:T(8,128)S(1)} %get-tuple-element.82), channel_id=1, replica_groups=mesh['dom'=8,'grp'=4] {'dom','grp'}, dimensions={0} | all-to-all | bytes 262144 | tf_op jit(solution)/shard_map/all_to_all | solution.py:303
  78.3 1.4 apply.10
  79.7 10.0 %all_to_all.91.refs_0_ = f32[32,8,128]{2,1,0:T(8,128)S(1)} all-to-all(f32[32,8,128]{2,1,0:T(8,128)S(1)} %get-tuple-element.83), channel_id=1, replica_groups=mesh['dom'=8,'grp'=4] {'dom','grp'}, dimensions={0} | all-to-all | bytes 262144 | tf_op jit(solution)/shard_map/all_to_all | solution.py:303
  89.7 0.2 update.9
  89.8 10.0 %all_to_all.92.recv_ref = f32[32,8,128]{2,1,0:T(8,128)S(1)} all-to-all(f32[32,8,128]{2,1,0:T(8,128)S(1)} %get-tuple-element.90), channel_id=1, replica_groups=mesh['dom'=8,'grp'=4] {'dom','grp'}, dimensions={0} | all-to-all | bytes 262144 | tf_op jit(solution)/shard_map/all_to_all | solution.py:303
  99.8 1.4 apply.11
  101.2 10.0 %all_to_all.93.refs_0_ = f32[32,8,128]{2,1,0:T(8,128)S(1)} all-to-all(f32[32,8,128]{2,1,0:T(8,128)S(1)} %get-tuple-element.91), channel_id=1, replica_groups=mesh['dom'=8,'grp'=4] {'dom','grp'}, dimensions={0} | all-to-all | bytes 262144 | tf_op jit(solution)/shard_map/all_to_all | solution.py:303
  111.2 0.2 update.10
  111.3 10.0 %all_to_all.94.recv_ref = f32[32,8,128]{2,1,0:T(8,128)S(1)} all-to-all(f32[32,8,128]{2,1,0:T(8,128)S(1)} %get-tuple-element.98), channel_id=1, replica_groups=mesh['dom'=8,'grp'=4] {'dom','grp'}, dimensions={0} | all-to-all | bytes 262144 | tf_op jit(solution)/shard_map/all_to_all | solution.py:303
  121.3 1.4 apply.12
  122.7 10.0 %all_to_all.95.refs_0_ = f32[32,8,128]{2,1,0:T(8,128)S(1)} all-to-all(f32[32,8,128]{2,1,0:T(8,128)S(1)} %get-tuple-element.99), channel_id=1, replica_groups=mesh['dom'=8,'grp'=4] {'dom','grp'}, dimensions={0} | all-to-all | bytes 262144 | tf_op jit(solution)/shard_map/all_to_all | solution.py:303
  132.6 0.2 update.11
  132.8 10.0 %all_to_all.96.recv_ref = f32[32,8,128]{2,1,0:T(8,128)S(1)} all-to-all(f32[32,8,128]{2,1,0:T(8,128)S(1)} %get-tuple-element.106), channel_id=1, replica_groups=mesh['dom'=8,'grp'=4] {'dom','grp'}, dimensions={0} | all-to-all | bytes 262144 | tf_op jit(solution)/shard_map/all_to_all | solution.py:303
  142.8 1.4 apply.13
  144.2 10.0 %all_to_all.97.refs_0_ = f32[32,8,128]{2,1,0:T(8,128)S(1)} all-to-all(f32[32,8,128]{2,1,0:T(8,128)S(1)} %get-tuple-element.107), channel_id=1, replica_groups=mesh['dom'=8,'grp'=4] {'dom','grp'}, dimensions={0} | all-to-all | bytes 262144 | tf_op jit(solution)/shard_map/all_to_all | solution.py:303
  154.1 0.2 update.12
  154.3 10.0 %all_to_all.98.recv_ref = f32[32,8,128]{2,1,0:T(8,128)S(1)} all-to-all(f32[32,8,128]{2,1,0:T(8,128)S(1)} %get-tuple-element.114), channel_id=1, replica_groups=mesh['dom'=8,'grp'=4] {'dom','grp'}, dimensions={0} | all-to-all | bytes 262144 | tf_op jit(solution)/shard_map/all_to_all | solution.py:303
  164.3 1.4 apply.14
  165.7 10.0 %all_to_all.99.refs_0_ = f32[32,8,128]{2,1,0:T(8,128)S(1)} all-to-all(f32[32,8,128]{2,1,0:T(8,128)S(1)} %get-tuple-element.115), channel_id=1, replica_groups=mesh['dom'=8,'grp'=4] {'dom','grp'}, dimensions={0} | all-to-all | bytes 262144 | tf_op jit(solution)/shard_map/all_to_all | solution.py:303
  175.6 0.8 update.13
  176.4 10.0 %all_to_all.100.recv_ref = f32[32,8,128]{2,1,0:T(8,128)S(1)} all-to-all(f32[32,8,128]{2,1,0:T(8,128)S(1)} %get-tuple-element.122), channel_id=1, replica_groups=mesh['dom'=8,'grp'=4] {'dom','grp'}, dimensions={0} | all-to-all | bytes 262144 | tf_op jit(solution)/shard_map/all_to_all | solution.py:303
  186.3 1.3 apply.15
  187.7 12.3 %all_to_all.101.recv_ref = f32[32,16,128]{2,1,0:T(8,128)S(1)} all-to-all(f32[32,16,128]{2,1,0:T(8,128)S(1)} %get-tuple-element.123), channel_id=1, replica_groups=mesh['dom'=8,'grp'=4] {'dom','grp'}, dimensions={0} | all-to-all | bytes 524288 | tf_op jit(solution)/shard_map/all_to_all | solution.py:303
  200.0 0.7 finish.1
  (1 shorter events, 0.0 us)
Async XLA Ops:
  0.6 2.0 copy-start
  2.6 1.0 copy-start.1
  3.6 0.7 copy-start.2
  4.3 0.7 copy-start.3
  5.1 0.7 copy-start.4
  5.8 0.7 copy-start.5
  6.5 0.7 copy-start.6
  7.1 0.7 copy-start.7

commit v4 on v3

--- a/solution.py
+++ b/solution.py
@@ -172,24 +172,27 @@
     r = plan.join(*(recv_ref[plan.base(0, lower) + me, : plan.rows, :] for lower in (False, True)))
     own_ref[...] = r
     slab_ref[full:tall, :] = jnp.zeros((tall - full, 3 * faces), jnp.float32)
-    pick_ref[...] = sum3(jnp.dot(parts3(slab_ref[...]), hot_ref[...], preferred_element_type=jnp.float32))
     wide = [jnp.broadcast_to(r[a : a + 1, :], (SUB, faces)) for a in range(width)]
     turn_ref[full:tall, :] = jnp.zeros((tall - full, slots * faces), jnp.float32)
+    for low in range(0, full, SUB):
+        high = min(low + SUB, full)
+        for s in range(slots):
+            turned = None
+            for a in range(width):
+                backward = blocks_ref[s, a, low:high, :] * wide[a][: high - low]
+                turned = backward if turned is None else turned + backward
+            turn_ref[low:high, s * faces : (s + 1) * faces] = turned
+    pick_ref[...] = sum3(jnp.dot(parts3(slab_ref[...]), hot_ref[...], preferred_element_type=jnp.float32))
+    slab_ref[...] = sum3(jnp.dot(parts3(turn_ref[...]), back_ref[...], preferred_element_type=jnp.float32))
     total = [None] * width
     for low in range(0, full, SUB):
         high = min(low + SUB, full)
         acc = [None] * width
         for s in range(slots):
-            cols = slice(s * faces, (s + 1) * faces)
-            picked = pick_ref[low:high, cols]
-            turned = None
+            picked = pick_ref[low:high, s * faces : (s + 1) * faces]
             for a in range(width):
-                tile = blocks_ref[s, a, low:high, :]
-                forward = tile * picked
-                backward = tile * wide[a][: high - low]
+                forward = blocks_ref[s, a, low:high, :] * picked
                 acc[a] = forward if acc[a] is None else acc[a] + forward
-                turned = backward if turned is None else turned + backward
-            turn_ref[low:high, cols] = turned
         for a in range(width):
             line = jnp.sum(acc[a], axis=0, keepdims=True)
             total[a] = line if total[a] is None else total[a] + line
@@ -203,7 +206,6 @@
         fold.append(line + pltpu.roll(line, faces // 4, 1))
     lane = lax.broadcasted_iota(jnp.int32, (1, faces), 1)
     line = jnp.where(lane < faces // 4 * 3, fold[0], fold[1])
-    slab_ref[...] = sum3(jnp.dot(parts3(turn_ref[...]), back_ref[...], preferred_element_type=jnp.float32))
     if last:
         for n in range(n_dom * n_grp):
             out_ref[n, width : width + 1, :] = line
@@ -271,7 +273,7 @@
     ro_ref[...] = own - alpha * (w + beta * before)
 
 
-def call(kernel, outs, args, scratch=(), name=None, space=pltpu.VMEM):
+def call(kernel, outs, args, scratch=(), name=None, space=pltpu.VMEM, grant=VMEM_GRANT):
     vmem = pl.BlockSpec(memory_space=pltpu.VMEM)
     return pl.pallas_call(
         kernel,
@@ -280,7 +282,7 @@
         out_specs=jax.tree.map(lambda _: vmem, outs),
         scratch_shapes=list(scratch),
         name=name,
-        compiler_params=pltpu.CompilerParams(vmem_limit_bytes=VMEM_GRANT),
+        compiler_params=pltpu.CompilerParams(vmem_limit_bytes=grant),
     )(*args)
 
 
@@ -313,7 +315,7 @@
             field,
             jax.ShapeDtypeStruct(blocks.shape, f32),
         ),
-        inputs + (diagonal, blocks),
+        tuple(pltpu.with_memory_space_constraint(a, pltpu.HBM) for a in inputs + (diagonal, blocks)),
         [pltpu.VMEM(a.shape, a.dtype) for a in inputs] + [slab, pltpu.SemaphoreType.DMA((len(inputs) + 2,))],
         name="rhs",
         space=pl.ANY,

time: 202 us -> 194 us (0.960)
  local copies, waits for them, and re-layouts: 7.18 us -> 0 us
    unnamed x16 -> x0, local copies, waits for them, and re-layouts: 7.18 us -> none
where the time goes in v4:
time: 194 us; the launch traced here: 193 us
  blocking collectives  177 us (91%)
  Pallas kernels  15.4 us (8%)
    all_to_all x17, blocking collectives, exchange(): return lax.all_to_all(v, ALL, 0, 0)  177 us
    pallas_call x18, Pallas kernels, call(): pl.pallas_call(kernel, out_shape=outs, in_specs=[pl.BlockSpec(memory_spac...  15.4 us

profile of v4, /device:TPU:0, one launch (start us, length us, event | category | flops | bytes accessed | tf_op | source)
XLA Modules:
  0.0 193.3 jit_solution(14254914033874514326)
XLA Ops:
  0.6 2.2 %rhs.1 = (f32[32,8,128]{2,1,0:T(8,128)S(1)}, bf16[384,896]{1,0:T(8,128)(2,1)S(1)}, bf16[896,384]{1,0:T(8,128)(2,1)S(1)}, f32[15,128]{1,0:T(8,128)S(1)}, f32[7,15,60,128]{3,2,1,0:T(8,128)S(1)}) custom-call(s32[7,128]{1,0:T(8,128)} %cols_hbm.1, s32[4,128]{1,0:T(4,128)} %owner_hbm.1, bf16[20,80,128]{2,1,0:T(8,128)(2,1)} %inv_hbm.1, bf16[80,128]{1,0:T(8,128)(2,1)} %load_hbm.1, ...), custom_call_target="tpu_custom_call" | custom-call | tf_op jit(solution)/shard_map/rhs/pallas_call | solution.py:278
  2.9 15.3 %all_to_all.85.recv_ref = f32[32,8,128]{2,1,0:T(8,128)S(1)} all-to-all(f32[32,8,128]{2,1,0:T(8,128)S(1)} %get-tuple-element.65), channel_id=1, replica_groups=mesh['dom'=8,'grp'=4] {'dom','grp'}, dimensions={0} | all-to-all | bytes 262144 | tf_op jit(solution)/shard_map/all_to_all | solution.py:305
  18.2 10.0 %all_to_all.86.recv_ref = f32[32,8,128]{2,1,0:T(8,128)S(1)} all-to-all(f32[32,8,128]{2,1,0:T(8,128)S(1)} %get-tuple-element.66), channel_id=1, replica_groups=mesh['dom'=8,'grp'=4] {'dom','grp'}, dimensions={0} | all-to-all | bytes 262144 | tf_op jit(solution)/shard_map/all_to_all | solution.py:305
  28.2 1.3 apply.8
  29.5 10.0 %all_to_all.87.refs_0_ = f32[32,8,128]{2,1,0:T(8,128)S(1)} all-to-all(f32[32,8,128]{2,1,0:T(8,128)S(1)} %get-tuple-element.71), channel_id=1, replica_groups=mesh['dom'=8,'grp'=4] {'dom','grp'}, dimensions={0} | all-to-all | bytes 262144 | tf_op jit(solution)/shard_map/all_to_all | solution.py:305
  39.5 0.1 update.7
  39.6 10.0 %all_to_all.88.recv_ref = f32[32,8,128]{2,1,0:T(8,128)S(1)} all-to-all(f32[32,8,128]{2,1,0:T(8,128)S(1)} %get-tuple-element.74), channel_id=1, replica_groups=mesh['dom'=8,'grp'=4] {'dom','grp'}, dimensions={0} | all-to-all | bytes 262144 | tf_op jit(solution)/shard_map/all_to_all | solution.py:305
  49.6 1.3 apply.9
  50.9 10.0 %all_to_all.89.refs_0_ = f32[32,8,128]{2,1,0:T(8,128)S(1)} all-to-all(f32[32,8,128]{2,1,0:T(8,128)S(1)} %get-tuple-element.75), channel_id=1, replica_groups=mesh['dom'=8,'grp'=4] {'dom','grp'}, dimensions={0} | all-to-all | bytes 262144 | tf_op jit(solution)/shard_map/all_to_all | solution.py:305
  60.9 0.2 update.8
  61.1 10.0 %all_to_all.90.recv_ref = f32[32,8,128]{2,1,0:T(8,128)S(1)} all-to-all(f32[32,8,128]{2,1,0:T(8,128)S(1)} %get-tuple-element.82), channel_id=1, replica_groups=mesh['dom'=8,'grp'=4] {'dom','grp'}, dimensions={0} | all-to-all | bytes 262144 | tf_op jit(solution)/shard_map/all_to_all | solution.py:305
  71.1 1.3 apply.10
  72.4 10.0 %all_to_all.91.refs_0_ = f32[32,8,128]{2,1,0:T(8,128)S(1)} all-to-all(f32[32,8,128]{2,1,0:T(8,128)S(1)} %get-tuple-element.83), channel_id=1, replica_groups=mesh['dom'=8,'grp'=4] {'dom','grp'}, dimensions={0} | all-to-all | bytes 262144 | tf_op jit(solution)/shard_map/all_to_all | solution.py:305
  82.4 0.2 update.9
  82.6 10.0 %all_to_all.92.recv_ref = f32[32,8,128]{2,1,0:T(8,128)S(1)} all-to-all(f32[32,8,128]{2,1,0:T(8,128)S(1)} %get-tuple-element.90), channel_id=1, replica_groups=mesh['dom'=8,'grp'=4] {'dom','grp'}, dimensions={0} | all-to-all | bytes 262144 | tf_op jit(solution)/shard_map/all_to_all | solution.py:305
  92.5 1.3 apply.11
  93.9 10.0 %all_to_all.93.refs_0_ = f32[32,8,128]{2,1,0:T(8,128)S(1)} all-to-all(f32[32,8,128]{2,1,0:T(8,128)S(1)} %get-tuple-element.91), channel_id=1, replica_groups=mesh['dom'=8,'grp'=4] {'dom','grp'}, dimensions={0} | all-to-all | bytes 262144 | tf_op jit(solution)/shard_map/all_to_all | solution.py:305
  103.9 0.2 update.10
  104.0 10.0 %all_to_all.94.recv_ref = f32[32,8,128]{2,1,0:T(8,128)S(1)} all-to-all(f32[32,8,128]{2,1,0:T(8,128)S(1)} %get-tuple-element.98), channel_id=1, replica_groups=mesh['dom'=8,'grp'=4] {'dom','grp'}, dimensions={0} | all-to-all | bytes 262144 | tf_op jit(solution)/shard_map/all_to_all | solution.py:305
  114.0 1.3 apply.12
  115.3 10.0 %all_to_all.95.refs_0_ = f32[32,8,128]{2,1,0:T(8,128)S(1)} all-to-all(f32[32,8,128]{2,1,0:T(8,128)S(1)} %get-tuple-element.99), channel_id=1, replica_groups=mesh['dom'=8,'grp'=4] {'dom','grp'}, dimensions={0} | all-to-all | bytes 262144 | tf_op jit(solution)/shard_map/all_to_all | solution.py:305
  125.3 0.2 update.11
  125.5 10.0 %all_to_all.96.recv_ref = f32[32,8,128]{2,1,0:T(8,128)S(1)} all-to-all(f32[32,8,128]{2,1,0:T(8,128)S(1)} %get-tuple-element.106), channel_id=1, replica_groups=mesh['dom'=8,'grp'=4] {'dom','grp'}, dimensions={0} | all-to-all | bytes 262144 | tf_op jit(solution)/shard_map/all_to_all | solution.py:305
  135.5 1.3 apply.13
  136.8 10.0 %all_to_all.97.refs_0_ = f32[32,8,128]{2,1,0:T(8,128)S(1)} all-to-all(f32[32,8,128]{2,1,0:T(8,128)S(1)} %get-tuple-element.107), channel_id=1, replica_groups=mesh['dom'=8,'grp'=4] {'dom','grp'}, dimensions={0} | all-to-all | bytes 262144 | tf_op jit(solution)/shard_map/all_to_all | solution.py:305
  146.8 0.2 update.12
  147.0 10.0 %all_to_all.98.recv_ref = f32[32,8,128]{2,1,0:T(8,128)S(1)} all-to-all(f32[32,8,128]{2,1,0:T(8,128)S(1)} %get-tuple-element.114), channel_id=1, replica_groups=mesh['dom'=8,'grp'=4] {'dom','grp'}, dimensions={0} | all-to-all | bytes 262144 | tf_op jit(solution)/shard_map/all_to_all | solution.py:305
  156.9 1.3 apply.14
  158.3 10.0 %all_to_all.99.refs_0_ = f32[32,8,128]{2,1,0:T(8,128)S(1)} all-to-all(f32[32,8,128]{2,1,0:T(8,128)S(1)} %get-tuple-element.115), channel_id=1, replica_groups=mesh['dom'=8,'grp'=4] {'dom','grp'}, dimensions={0} | all-to-all | bytes 262144 | tf_op jit(solution)/shard_map/all_to_all | solution.py:305
  168.2 0.8 update.13
  169.0 10.0 %all_to_all.100.recv_ref = f32[32,8,128]{2,1,0:T(8,128)S(1)} all-to-all(f32[32,8,128]{2,1,0:T(8,128)S(1)} %get-tuple-element.122), channel_id=1, replica_groups=mesh['dom'=8,'grp'=4] {'dom','grp'}, dimensions={0} | all-to-all | bytes 262144 | tf_op jit(solution)/shard_map/all_to_all | solution.py:305
  179.0 1.3 apply.15
  180.2 12.3 %all_to_all.101.recv_ref = f32[32,16,128]{2,1,0:T(8,128)S(1)} all-to-all(f32[32,16,128]{2,1,0:T(8,128)S(1)} %get-tuple-element.123), channel_id=1, replica_groups=mesh['dom'=8,'grp'=4] {'dom','grp'}, dimensions={0} | all-to-all | bytes 524288 | tf_op jit(solution)/shard_map/all_to_all | solution.py:305
  192.6 0.7 finish.1
  (1 shorter events, 0.0 us)

commit v5 on v4

--- a/solution.py
+++ b/solution.py
@@ -11,23 +11,24 @@
 SUB = 8
 ALL = ("dom", "grp")
 VMEM_GRANT = 16 * 1024 * 1024
+PARTS = 3
 
 
 def up(n, m):
     return (n + m - 1) // m * m
 
 
-def parts3(x):
-    hi = x.astype(jnp.bfloat16)
-    rest = x - hi.astype(jnp.float32)
-    mid = rest.astype(jnp.bfloat16)
-    low = (rest - mid.astype(jnp.float32)).astype(jnp.bfloat16)
-    return jnp.concatenate([hi, mid, low], axis=0)
-
-
-def sum3(y):
-    n = y.shape[0] // 3
-    return y[:n] + y[n : 2 * n] + y[2 * n :]
+def parts(x, count):
+    out = [x.astype(jnp.bfloat16)]
+    while len(out) < count:
+        x = x - out[-1].astype(jnp.float32)
+        out.append(x.astype(jnp.bfloat16))
+    return jnp.concatenate(out, axis=0)
+
+
+def whole(y, count):
+    n = y.shape[0] // count
+    return sum((y[k * n : (k + 1) * n] for k in range(1, count)), y[:n])
 
 
 class Plan:
@@ -144,9 +145,9 @@
     for k in range(sides):
         entry = -lifted[k * full : (k + 1) * full] * area_ref[k : k + 1, :]
         entry = jnp.concatenate([entry, jnp.zeros((pad, entry.shape[1]), jnp.float32)], axis=0)
-        part = jnp.dot(parts3(entry), scatter_of(slots + k), preferred_element_type=jnp.float32)
+        part = jnp.dot(parts(entry, 3), scatter_of(slots + k), preferred_element_type=jnp.float32)
         total = part if total is None else total + part
-    slab_ref[...] = sum3(total)
+    slab_ref[...] = whole(total, 3)
     plan.post(out_ref, slab_ref, jnp.zeros((1, faces), jnp.float32))
     for fetch in fetches[6:]:
         fetch.wait()
@@ -174,29 +175,40 @@
     slab_ref[full:tall, :] = jnp.zeros((tall - full, 3 * faces), jnp.float32)
     wide = [jnp.broadcast_to(r[a : a + 1, :], (SUB, faces)) for a in range(width)]
     turn_ref[full:tall, :] = jnp.zeros((tall - full, slots * faces), jnp.float32)
-    for low in range(0, full, SUB):
-        high = min(low + SUB, full)
-        for s in range(slots):
-            turned = None
-            for a in range(width):
-                backward = blocks_ref[s, a, low:high, :] * wide[a][: high - low]
-                turned = backward if turned is None else turned + backward
-            turn_ref[low:high, s * faces : (s + 1) * faces] = turned
-    pick_ref[...] = sum3(jnp.dot(parts3(slab_ref[...]), hot_ref[...], preferred_element_type=jnp.float32))
-    slab_ref[...] = sum3(jnp.dot(parts3(turn_ref[...]), back_ref[...], preferred_element_type=jnp.float32))
-    total = [None] * width
-    for low in range(0, full, SUB):
-        high = min(low + SUB, full)
-        acc = [None] * width
-        for s in range(slots):
-            picked = pick_ref[low:high, s * faces : (s + 1) * faces]
-            for a in range(width):
-                forward = blocks_ref[s, a, low:high, :] * picked
-                acc[a] = forward if acc[a] is None else acc[a] + forward
-        for a in range(width):
-            line = jnp.sum(acc[a], axis=0, keepdims=True)
-            total[a] = line if total[a] is None else total[a] + line
-    forward = jnp.concatenate(total, axis=0)
+    window = parts(slab_ref[...], PARTS)
+    groups = [slice(s * faces, min(s + 2, slots) * faces) for s in range(0, slots, 2)]
+
+    def gather(at):
+        picked = jnp.dot(window, hot_ref[:, at], preferred_element_type=jnp.float32)
+        pick_ref[:, at] = whole(picked, PARTS)
+
+    acc, rest, back = [None] * width, [None] * width, None
+    gather(groups[0])
+    for n, at in enumerate(groups):
+        if n + 1 < len(groups):
+            gather(groups[n + 1])
+        for low in range(0, full, SUB):
+            high = min(low + SUB, full)
+            held = acc if high - low == SUB else rest
+            for s in range(at.start // faces, at.stop // faces):
+                cols = slice(s * faces, (s + 1) * faces)
+                picked = pick_ref[low:high, cols]
+                turned = None
+                for a in range(width):
+                    tile = blocks_ref[s, a, low:high, :]
+                    forward = tile * picked
+                    backward = tile * wide[a][: high - low]
+                    held[a] = forward if held[a] is None else held[a] + forward
+                    turned = backward if turned is None else turned + backward
+                turn_ref[low:high, cols] = turned
+        part = jnp.dot(parts(turn_ref[:, at], PARTS), back_ref[at, :], preferred_element_type=jnp.float32)
+        back = part if back is None else back + part
+    slab_ref[...] = whole(back, PARTS)
+    lines = []
+    for a in range(width):
+        line = jnp.sum(acc[a], axis=0, keepdims=True)
+        lines.append(line if rest[a] is None else line + jnp.sum(rest[a], axis=0, keepdims=True))
+    forward = jnp.concatenate(lines, axis=0)
     plain = diag_ref[...] * r + forward
     square = jnp.sum(r * r, axis=0, keepdims=True)
     cross = jnp.sum(r * (plain + forward), axis=0, keepdims=True)

time: 194 us -> 192 us (0.990)
  no operation moved by 1% of the time
where the time goes in v5:
time: 192 us; the launch traced here: 191 us
  blocking collectives  177 us (92%)
  Pallas kernels  13.5 us (7%)
    all_to_all x17, blocking collectives, exchange(): return lax.all_to_all(v, ALL, 0, 0)  177 us
    pallas_call x18, Pallas kernels, call(): pl.pallas_call(kernel, out_shape=outs, in_specs=[pl.BlockSpec(memory_spac...  13.5 us

profile of v5, /device:TPU:0, one launch (start us, length us, event | category | flops | bytes accessed | tf_op | source)
XLA Modules:
  0.0 191.4 jit_solution(12859154518509336777)
XLA Ops:
  0.6 2.2 %rhs.1 = (f32[32,8,128]{2,1,0:T(8,128)S(1)}, bf16[384,896]{1,0:T(8,128)(2,1)S(1)}, bf16[896,384]{1,0:T(8,128)(2,1)S(1)}, f32[15,128]{1,0:T(8,128)S(1)}, f32[7,15,60,128]{3,2,1,0:T(8,128)S(1)}) custom-call(s32[7,128]{1,0:T(8,128)} %cols_hbm.1, s32[4,128]{1,0:T(4,128)} %owner_hbm.1, bf16[20,80,128]{2,1,0:T(8,128)(2,1)} %inv_hbm.1, bf16[80,128]{1,0:T(8,128)(2,1)} %load_hbm.1, ...), custom_call_target="tpu_custom_call" | custom-call | tf_op jit(solution)/shard_map/rhs/pallas_call | solution.py:290
  2.9 15.3 %all_to_all.85.recv_ref = f32[32,8,128]{2,1,0:T(8,128)S(1)} all-to-all(f32[32,8,128]{2,1,0:T(8,128)S(1)} %get-tuple-element.65), channel_id=1, replica_groups=mesh['dom'=8,'grp'=4] {'dom','grp'}, dimensions={0} | all-to-all | bytes 262144 | tf_op jit(solution)/shard_map/all_to_all | solution.py:317
  18.2 10.0 %all_to_all.86.recv_ref = f32[32,8,128]{2,1,0:T(8,128)S(1)} all-to-all(f32[32,8,128]{2,1,0:T(8,128)S(1)} %get-tuple-element.66), channel_id=1, replica_groups=mesh['dom'=8,'grp'=4] {'dom','grp'}, dimensions={0} | all-to-all | bytes 262144 | tf_op jit(solution)/shard_map/all_to_all | solution.py:317
  28.2 1.1 apply.8
  29.3 10.0 %all_to_all.87.refs_0_ = f32[32,8,128]{2,1,0:T(8,128)S(1)} all-to-all(f32[32,8,128]{2,1,0:T(8,128)S(1)} %get-tuple-element.71), channel_id=1, replica_groups=mesh['dom'=8,'grp'=4] {'dom','grp'}, dimensions={0} | all-to-all | bytes 262144 | tf_op jit(solution)/shard_map/all_to_all | solution.py:317
  39.3 0.1 update.7
  39.4 10.0 %all_to_all.88.recv_ref = f32[32,8,128]{2,1,0:T(8,128)S(1)} all-to-all(f32[32,8,128]{2,1,0:T(8,128)S(1)} %get-tuple-element.74), channel_id=1, replica_groups=mesh['dom'=8,'grp'=4] {'dom','grp'}, dimensions={0} | all-to-all | bytes 262144 | tf_op jit(solution)/shard_map/all_to_all | solution.py:317
  49.3 1.1 apply.9
  50.5 10.0 %all_to_all.89.refs_0_ = f32[32,8,128]{2,1,0:T(8,128)S(1)} all-to-all(f32[32,8,128]{2,1,0:T(8,128)S(1)} %get-tuple-element.75), channel_id=1, replica_groups=mesh['dom'=8,'grp'=4] {'dom','grp'}, dimensions={0} | all-to-all | bytes 262144 | tf_op jit(solution)/shard_map/all_to_all | solution.py:317
  60.4 0.2 update.8
  60.6 10.0 %all_to_all.90.recv_ref = f32[32,8,128]{2,1,0:T(8,128)S(1)} all-to-all(f32[32,8,128]{2,1,0:T(8,128)S(1)} %get-tuple-element.82), channel_id=1, replica_groups=mesh['dom'=8,'grp'=4] {'dom','grp'}, dimensions={0} | all-to-all | bytes 262144 | tf_op jit(solution)/shard_map/all_to_all | solution.py:317
  70.6 1.1 apply.10
  71.7 10.0 %all_to_all.91.refs_0_ = f32[32,8,128]{2,1,0:T(8,128)S(1)} all-to-all(f32[32,8,128]{2,1,0:T(8,128)S(1)} %get-tuple-element.83), channel_id=1, replica_groups=mesh['dom'=8,'grp'=4] {'dom','grp'}, dimensions={0} | all-to-all | bytes 262144 | tf_op jit(solution)/shard_map/all_to_all | solution.py:317
  81.6 0.2 update.9
  81.8 10.0 %all_to_all.92.recv_ref = f32[32,8,128]{2,1,0:T(8,128)S(1)} all-to-all(f32[32,8,128]{2,1,0:T(8,128)S(1)} %get-tuple-element.90), channel_id=1, replica_groups=mesh['dom'=8,'grp'=4] {'dom','grp'}, dimensions={0} | all-to-all | bytes 262144 | tf_op jit(solution)/shard_map/all_to_all | solution.py:317
  91.8 1.1 apply.11
  92.9 10.0 %all_to_all.93.refs_0_ = f32[32,8,128]{2,1,0:T(8,128)S(1)} all-to-all(f32[32,8,128]{2,1,0:T(8,128)S(1)} %get-tuple-element.91), channel_id=1, replica_groups=mesh['dom'=8,'grp'=4] {'dom','grp'}, dimensions={0} | all-to-all | bytes 262144 | tf_op jit(solution)/shard_map/all_to_all | solution.py:317
  102.9 0.2 update.10
  103.0 10.0 %all_to_all.94.recv_ref = f32[32,8,128]{2,1,0:T(8,128)S(1)} all-to-all(f32[32,8,128]{2,1,0:T(8,128)S(1)} %get-tuple-element.98), channel_id=1, replica_groups=mesh['dom'=8,'grp'=4] {'dom','grp'}, dimensions={0} | all-to-all | bytes 262144 | tf_op jit(solution)/shard_map/all_to_all | solution.py:317
  113.0 1.1 apply.12
  114.1 10.0 %all_to_all.95.refs_0_ = f32[32,8,128]{2,1,0:T(8,128)S(1)} all-to-all(f32[32,8,128]{2,1,0:T(8,128)S(1)} %get-tuple-element.99), channel_id=1, replica_groups=mesh['dom'=8,'grp'=4] {'dom','grp'}, dimensions={0} | all-to-all | bytes 262144 | tf_op jit(solution)/shard_map/all_to_all | solution.py:317
  124.1 0.2 update.11
  124.3 10.0 %all_to_all.96.recv_ref = f32[32,8,128]{2,1,0:T(8,128)S(1)} all-to-all(f32[32,8,128]{2,1,0:T(8,128)S(1)} %get-tuple-element.106), channel_id=1, replica_groups=mesh['dom'=8,'grp'=4] {'dom','grp'}, dimensions={0} | all-to-all | bytes 262144 | tf_op jit(solution)/shard_map/all_to_all | solution.py:317
  134.2 1.1 apply.13
  135.3 10.0 %all_to_all.97.refs_0_ = f32[32,8,128]{2,1,0:T(8,128)S(1)} all-to-all(f32[32,8,128]{2,1,0:T(8,128)S(1)} %get-tuple-element.107), channel_id=1, replica_groups=mesh['dom'=8,'grp'=4] {'dom','grp'}, dimensions={0} | all-to-all | bytes 262144 | tf_op jit(solution)/shard_map/all_to_all | solution.py:317
  145.3 0.2 update.12
  145.5 10.0 %all_to_all.98.recv_ref = f32[32,8,128]{2,1,0:T(8,128)S(1)} all-to-all(f32[32,8,128]{2,1,0:T(8,128)S(1)} %get-tuple-element.114), channel_id=1, replica_groups=mesh['dom'=8,'grp'=4] {'dom','grp'}, dimensions={0} | all-to-all | bytes 262144 | tf_op jit(solution)/shard_map/all_to_all | solution.py:317
  155.4 1.1 apply.14
  156.6 10.0 %all_to_all.99.refs_0_ = f32[32,8,128]{2,1,0:T(8,128)S(1)} all-to-all(f32[32,8,128]{2,1,0:T(8,128)S(1)} %get-tuple-element.115), channel_id=1, replica_groups=mesh['dom'=8,'grp'=4] {'dom','grp'}, dimensions={0} | all-to-all | bytes 262144 | tf_op jit(solution)/shard_map/all_to_all | solution.py:317
  166.5 0.8 update.13
  167.3 10.0 %all_to_all.100.recv_ref = f32[32,8,128]{2,1,0:T(8,128)S(1)} all-to-all(f32[32,8,128]{2,1,0:T(8,128)S(1)} %get-tuple-element.122), channel_id=1, replica_groups=mesh['dom'=8,'grp'=4] {'dom','grp'}, dimensions={0} | all-to-all | bytes 262144 | tf_op jit(solution)/shard_map/all_to_all | solution.py:317
  177.2 1.1 apply.15
  178.3 12.3 %all_to_all.101.recv_ref = f32[32,16,128]{2,1,0:T(8,128)S(1)} all-to-all(f32[32,16,128]{2,1,0:T(8,128)S(1)} %get-tuple-element.123), channel_id=1, replica_groups=mesh['dom'=8,'grp'=4] {'dom','grp'}, dimensions={0} | all-to-all | bytes 524288 | tf_op jit(solution)/shard_map/all_to_all | solution.py:317
  190.7 0.7 finish.1
  (1 shorter events, 0.0 us)

commit v6 on v5

--- a/solution.py
+++ b/solution.py
@@ -35,61 +35,69 @@
     def __init__(self, width, faces):
         self.n_dom, self.n_grp = lax.axis_size("dom"), lax.axis_size("grp")
         self.width, self.faces = width, faces
-        self.half = width // 2
-        self.rows = self.half + 1
-        self.tall = up(self.rows, SUB)
-
-    def base(self, shift, lower):
-        shift += self.n_dom // 2 if lower else 0
-        return lax.rem(lax.axis_index("dom") + (shift + self.n_dom), self.n_dom) * self.n_grp
-
-    def kept(self, shift):
-        return self.base(shift - self.n_dom // 2, False)
-
-    def left(self):
-        return lax.broadcasted_iota(jnp.int32, (1, self.faces), 1) < self.faces // 2
-
-    def split(self, rows, line):
-        h, left = self.half, self.left()
-        middle = rows[h : h + 1]
-        upper = jnp.where(left, middle, line)
-        lower = jnp.where(left, pltpu.roll(middle, self.faces // 2, 1), line)
-        return (
-            jnp.concatenate([rows[:h], upper], axis=0),
-            jnp.concatenate([rows[h + 1 :], lower], axis=0),
-        )
-
-    def join(self, upper, lower):
-        h = self.half
-        middle = jnp.where(self.left(), upper[h : h + 1], pltpu.roll(lower[h : h + 1], self.faces // 2, 1))
-        return jnp.concatenate([upper[:h], middle, lower[:h]], axis=0)
-
-    def post(self, out_ref, slab_ref, line):
-        w, f = self.width, self.faces
+        self.step = faces // SUB
+        self.dom = lax.axis_index("dom")
+        self.lane = lax.broadcasted_iota(jnp.int32, (2, faces), 1)
+        self.row = lax.broadcasted_iota(jnp.int32, (2, faces), 0)
+
+    def wrap(self, n):
+        return lax.rem(n + self.n_dom, self.n_dom)
+
+    def owners(self, t):
+        return lax.div(self.wrap(self.dom + (t - 1)), SUB) * (SUB * self.n_grp)
+
+    def first(self):
+        return lax.div(self.dom, SUB) * SUB
+
+    def peer(self, i, t):
+        return self.wrap(self.first() + (i + 1 - t)) * self.n_grp
+
+    def free(self, j):
+        cut = self.faces - self.step * j
+        return (self.row == 1) & (self.lane >= cut - self.step) & (self.lane < cut)
+
+    def post(self, out_ref, rows_of, line):
         for t in range(3):
+            base = self.owners(t)
             for q in range(self.n_grp):
-                rows = slab_ref[q * w : (q + 1) * w, t * f : (t + 1) * f]
-                for lower, piece in enumerate(self.split(rows, line)):
-                    out_ref[self.base(t - 1, lower) + q, : self.rows, :] = piece
+                rows = rows_of(t, q)
+                rows = jnp.concatenate([rows, jnp.zeros((2 * SUB - self.width, self.faces), jnp.float32)], axis=0)
+                for j in range(SUB):
+                    share = rows[2 * j : 2 * j + 2]
+                    if j:
+                        share = jnp.where(self.lane < self.faces - self.step * j, share, rows[2 * j - 1 : 2 * j + 1])
+                    if line is not None and t == 0:
+                        share = jnp.where(self.free(j), line, share)
+                    out_ref[base + (j * self.n_grp + q), t] = share
+
+    def join(self, recv_ref, t, q):
+        base = self.owners(t)
+        shares = [recv_ref[base + j * self.n_grp + q, t] for j in range(SUB)]
+        rows = []
+        for j, share in enumerate(shares):
+            below = shares[j + 1][0:1] if j + 1 < SUB else share[1:2]
+            shifted = jnp.concatenate([share[1:2], below], axis=0)
+            cut = self.faces - self.step * j
+            rows.append(jnp.where(self.lane < cut - self.step * self.row, share, shifted))
+        return jnp.concatenate(rows, axis=0)[: self.width]
 
     def owned(self, recv_ref):
+        clear = self.free(lax.rem(self.dom, SUB))
         sums = []
-        for first in (functools.partial(self.base, lower=False), self.kept):
+        for i in range(SUB):
             total = None
             for t in range(3):
                 for q in range(self.n_grp):
-                    piece = recv_ref[first(t - 1) + q, : self.rows, :]
+                    piece = recv_ref[self.peer(i, t) + q, t]
                     total = piece if total is None else total + piece
-            row = lax.broadcasted_iota(jnp.int32, (self.rows, self.faces), 0)
-            lane = lax.broadcasted_iota(jnp.int32, (self.rows, self.faces), 1)
-            sums.append(jnp.where((row < self.half) | (lane < self.faces // 2), total, 0.0))
+            sums.append(jnp.where(clear, 0.0, total))
         return sums
 
-    def spread(self, out_ref, halves):
-        for first, piece in zip((functools.partial(self.base, lower=False), self.kept), halves):
+    def spread(self, out_ref, shares):
+        for i, share in enumerate(shares):
             for t in range(3):
                 for q in range(self.n_grp):
-                    out_ref[first(t - 1) + q, : self.rows, :] = piece
+                    out_ref[self.peer(i, t) + q, t] = share
 
 
 def rhs_kernel(width, cols_hbm, owner_hbm, inv_hbm, load_hbm, lift_hbm, area_hbm, diag_hbm, blocks_hbm, out_ref, hot_ref, back_ref, diag_ref, blocks_ref, cols_ref, owner_ref, inv_ref, load_ref, lift_ref, area_ref, slab_ref, sems):
@@ -104,7 +112,7 @@
     ]
     for fetch in fetches:
         fetch.start()
-    faces = out_ref.shape[2]
+    faces = out_ref.shape[-1]
     plan = Plan(width, faces)
     full = width * plan.n_grp
     slots, sides = cols_ref.shape[0], owner_ref.shape[0]
@@ -148,16 +156,17 @@
         part = jnp.dot(parts(entry, 3), scatter_of(slots + k), preferred_element_type=jnp.float32)
         total = part if total is None else total + part
     slab_ref[...] = whole(total, 3)
-    plan.post(out_ref, slab_ref, jnp.zeros((1, faces), jnp.float32))
+    plan.post(out_ref, lambda t, q: slab_ref[q * width : (q + 1) * width, t * faces : (t + 1) * faces], None)
     for fetch in fetches[6:]:
         fetch.wait()
 
 
 def start_kernel(width, recv_ref, out_ref, r_ref):
-    plan = Plan(width, recv_ref.shape[2])
-    halves = plan.owned(recv_ref)
-    plan.spread(out_ref, halves)
-    r_ref[...] = jnp.stack(halves)
+    plan = Plan(width, recv_ref.shape[-1])
+    shares = plan.owned(recv_ref)
+    plan.spread(out_ref, shares)
+    for i, share in enumerate(shares):
+        r_ref[i] = share
 
 
 def apply_kernel(last, recv_ref, diag_ref, blocks_ref, hot_ref, back_ref, out_ref, own_ref, slab_ref, pick_ref, turn_ref):
@@ -167,10 +176,9 @@
     tall = slab_ref.shape[0]
     for t in range(3):
         for q in range(n_grp):
-            rows = plan.join(*(recv_ref[plan.base(t - 1, lower) + q, : plan.rows, :] for lower in (False, True)))
-            slab_ref[q * width : (q + 1) * width, t * faces : (t + 1) * faces] = rows
+            slab_ref[q * width : (q + 1) * width, t * faces : (t + 1) * faces] = plan.join(recv_ref, t, q)
     me = lax.axis_index("grp")
-    r = plan.join(*(recv_ref[plan.base(0, lower) + me, : plan.rows, :] for lower in (False, True)))
+    r = plan.join(recv_ref, 1, me)
     own_ref[...] = r
     slab_ref[full:tall, :] = jnp.zeros((tall - full, 3 * faces), jnp.float32)
     wide = [jnp.broadcast_to(r[a : a + 1, :], (SUB, faces)) for a in range(width)]
@@ -214,34 +222,38 @@
     cross = jnp.sum(r * (plain + forward), axis=0, keepdims=True)
     fold = []
     for line in (square, cross):
-        line = line + pltpu.roll(line, faces // 2, 1)
-        fold.append(line + pltpu.roll(line, faces // 4, 1))
+        shift = faces // 2
+        while shift * 2 >= plan.step:
+            line = line + pltpu.roll(line, shift, 1)
+            shift //= 2
+        fold.append(line)
     lane = lax.broadcasted_iota(jnp.int32, (1, faces), 1)
-    line = jnp.where(lane < faces // 4 * 3, fold[0], fold[1])
+    line = jnp.where(lax.rem(lane, plan.step) < plan.step // 2, fold[0], fold[1])
+
+    def rows_of(t, q):
+        rows = slab_ref[q * width : (q + 1) * width, t * faces : (t + 1) * faces]
+        return rows + jnp.where(me == q, plain, 0.0) if t == 1 else rows
+
     if last:
         for n in range(n_dom * n_grp):
             out_ref[n, width : width + 1, :] = line
         for t in range(3):
+            base = plan.wrap(plan.dom + (t - 1)) * n_grp
             for q in range(n_grp):
-                rows = slab_ref[q * width : (q + 1) * width, t * faces : (t + 1) * faces]
-                out_ref[plan.base(t - 1, False) + q, :width, :] = rows
-        mine = plan.base(0, False) + me
-        out_ref[mine, :width, :] = out_ref[mine, :width, :] + plain
+                out_ref[base + q, :width, :] = rows_of(t, q)
         return
-    for n in range(n_dom * n_grp):
-        out_ref[n, plan.half : plan.rows, :] = line
-    plan.post(out_ref, slab_ref, line)
-    for lower, piece in enumerate(plan.split(plain, jnp.zeros((1, faces), jnp.float32))):
-        mine = plan.base(0, lower) + me
-        out_ref[mine, : plan.rows, :] = out_ref[mine, : plan.rows, :] + piece
-
-
-def scalars(lines, faces, scal_ref):
-    lines = jnp.sum(lines, axis=0, keepdims=True)
-    lane = lax.broadcasted_iota(jnp.int32, (1, faces), 1)
-    norm_at = (lane >= faces // 2) & (lane < faces // 4 * 3)
-    norm = jnp.sum(jnp.where(norm_at, lines, 0.0), axis=1, keepdims=True)
-    cross = jnp.sum(jnp.where(lane >= faces // 4 * 3, lines, 0.0), axis=1, keepdims=True)
+    if n_dom > SUB:
+        for n in range(n_dom * n_grp):
+            out_ref[n, 0] = jnp.broadcast_to(line, (2, faces))
+    plan.post(out_ref, rows_of, line)
+
+
+def scalars(lines, start, step, scal_ref):
+    line = jnp.sum(lines, axis=0, keepdims=True)
+    lane = lax.broadcasted_iota(jnp.int32, line.shape, 1)
+    middle = start + step // 2
+    norm = jnp.sum(jnp.where((lane >= start) & (lane < middle), line, 0.0), axis=1, keepdims=True)
+    cross = jnp.sum(jnp.where((lane >= middle) & (lane < start + step), line, 0.0), axis=1, keepdims=True)
     if scal_ref is None:
         return norm, norm / cross, None
     beta = norm / scal_ref[0:1, 0:1]
@@ -254,18 +266,19 @@
     out_ref, ro_ref, so_ref, po_ref, xo_ref, scalo_ref = refs[-6:]
     faces = own_ref.shape[1]
     plan = Plan(width, faces)
-    norm, alpha, beta = scalars(recv_ref[:, plan.half, :], faces, scal_ref)
+    start = faces - plan.step * (lax.rem(plan.dom, SUB) + 1)
+    norm, alpha, beta = scalars(recv_ref[:, 0, 1, :], start, plan.step, scal_ref)
+    shares = []
+    for i, w in enumerate(plan.owned(recv_ref)):
+        s = w if first else w + beta * s_ref[i]
+        so_ref[i] = s
+        shares.append(r_ref[i] - alpha * s)
+        ro_ref[i] = shares[i]
+    plan.spread(out_ref, shares)
     own = own_ref[...]
     p = own if first else own + beta * p_ref[...]
     po_ref[...] = p
     xo_ref[...] = alpha * p if first else x_ref[...] + alpha * p
-    halves = []
-    for n, w in enumerate(plan.owned(recv_ref)):
-        s = w if first else w + beta * s_ref[n]
-        so_ref[n] = s
-        halves.append(r_ref[n] - alpha * s)
-        ro_ref[n] = halves[n]
-    plan.spread(out_ref, halves)
     scalo_ref[0:1, :] = jnp.broadcast_to(norm, (1, faces))
     scalo_ref[1:2, :] = jnp.broadcast_to(alpha, (1, faces))
 
@@ -273,11 +286,11 @@
 def finish_kernel(width, recv_ref, own_ref, past_ref, p_ref, x_ref, scal_ref, xo_ref, ro_ref):
     faces = own_ref.shape[1]
     plan = Plan(width, faces)
-    _, alpha, beta = scalars(recv_ref[:, width, :], faces, scal_ref)
+    _, alpha, beta = scalars(recv_ref[:, width, :], 0, plan.step, scal_ref)
     w = None
     for t in range(3):
         for q in range(plan.n_grp):
-            piece = recv_ref[plan.base(t - 1, False) + q, :width, :]
+            piece = recv_ref[plan.wrap(plan.dom + (t - 1)) * plan.n_grp + q, :width, :]
             w = piece if w is None else w + piece
     own = own_ref[...]
     before = (past_ref[...] - own) / scal_ref[1:2, 0:1]
@@ -303,15 +316,14 @@
 ):
     n_dom, n_grp = lax.axis_size("dom"), lax.axis_size("grp")
     slots, width, full, faces = blocks.shape
-    if width % 2 == 0 or n_dom < 6:
+    if width >= 2 * SUB or n_dom % SUB or faces % (16 * SUB):
         raise ValueError("unsupported split")
     tall = up(full, 16)
     f32 = jnp.float32
-    plan = Plan(width, faces)
-    pieces = jax.ShapeDtypeStruct((n_dom * n_grp, plan.tall, faces), f32)
+    pieces = jax.ShapeDtypeStruct((n_dom * n_grp, 3, 2, faces), f32)
     wide_pieces = jax.ShapeDtypeStruct((n_dom * n_grp, up(width + 1, SUB), faces), f32)
     field = jax.ShapeDtypeStruct((width, faces), f32)
-    halves = jax.ShapeDtypeStruct((2, plan.rows, faces), f32)
+    shares = jax.ShapeDtypeStruct((SUB, 2, faces), f32)
 
     def exchange(v):
         return lax.all_to_all(v, ALL, 0, 0)
@@ -332,7 +344,7 @@
         name="rhs",
         space=pl.ANY,
     )
-    sent, r = call(functools.partial(start_kernel, width), (pieces, halves), (exchange(sent),), name="start")
+    sent, r = call(functools.partial(start_kernel, width), (pieces, shares), (exchange(sent),), name="start")
     past, state = None, ()
     for iteration in range(ITERS):
         first, last = iteration == 0, iteration + 1 == ITERS
@@ -351,7 +363,7 @@
             )
         sent, r, *state = call(
             functools.partial(update_kernel, first, width),
-            (pieces, halves, halves, field, field, jax.ShapeDtypeStruct((2, faces), f32)),
+            (pieces, shares, shares, field, field, jax.ShapeDtypeStruct((2, faces), f32)),
             (got, own, r) + tuple(state),
             name="update",
         )

time: 192 us -> 185 us (0.964)
  blocking collectives: 177 us -> 169 us
    all_to_all x17, blocking collectives: 177 us -> 169 us  [exchange(): return lax.all_to_all(v, ALL, 0, 0)]
where the time goes in v6:
time: 185 us
  blocking collectives  169 us (91%)
  Pallas kernels  14.9 us (8%)
    all_to_all x17, blocking collectives, exchange(): return lax.all_to_all(v, ALL, 0, 0)  169 us
    pallas_call x18, Pallas kernels, call(): pl.pallas_call(kernel, out_shape=outs, in_specs=[pl.BlockSpec(memory_spac...  14.9 us

profile of v6, /device:TPU:0, one launch (start us, length us, event | category | flops | bytes accessed | tf_op | source)
XLA Modules:
  0.0 185.0 jit_solution(10778323917697312506)
XLA Ops:
  0.6 2.2 %rhs.1 = (f32[32,3,2,128]{3,2,1,0:T(2,128)S(1)}, bf16[384,896]{1,0:T(8,128)(2,1)S(1)}, bf16[896,384]{1,0:T(8,128)(2,1)S(1)}, f32[15,128]{1,0:T(8,128)S(1)}, f32[7,15,60,128]{3,2,1,0:T(8,128)S(1)}) custom-call(s32[7,128]{1,0:T(8,128)} %cols_hbm.1, s32[4,128]{1,0:T(4,128)} %owner_hbm.1, bf16[20,80,128]{2,1,0:T(8,128)(2,1)} %inv_hbm.1, ...), custom_call_target="tpu_custom_call" | custom-call | tf_op jit(solution)/shard_map/rhs/pallas_call | solution.py:303
  2.9 14.9 %all_to_all.85.recv_ref = f32[32,3,2,128]{3,2,1,0:T(2,128)S(1)} all-to-all(f32[32,3,2,128]{3,2,1,0:T(2,128)S(1)} %get-tuple-element.65), channel_id=1, replica_groups=mesh['dom'=8,'grp'=4] {'dom','grp'}, dimensions={0} | all-to-all | bytes 196608 | tf_op jit(solution)/shard_map/all_to_all | solution.py:329
  17.8 0.1 start.1
  17.8 9.5 %all_to_all.86.recv_ref = f32[32,3,2,128]{3,2,1,0:T(2,128)S(1)} all-to-all(f32[32,3,2,128]{3,2,1,0:T(2,128)S(1)} %get-tuple-element.66), channel_id=1, replica_groups=mesh['dom'=8,'grp'=4] {'dom','grp'}, dimensions={0} | all-to-all | bytes 196608 | tf_op jit(solution)/shard_map/all_to_all | solution.py:329
  27.3 1.2 apply.8
  28.6 9.5 %all_to_all.87.refs_0_ = f32[32,3,2,128]{3,2,1,0:T(2,128)S(1)} all-to-all(f32[32,3,2,128]{3,2,1,0:T(2,128)S(1)} %get-tuple-element.71), channel_id=1, replica_groups=mesh['dom'=8,'grp'=4] {'dom','grp'}, dimensions={0} | all-to-all | bytes 196608 | tf_op jit(solution)/shard_map/all_to_all | solution.py:329
  38.1 0.1 update.7
  38.2 9.5 %all_to_all.88.recv_ref = f32[32,3,2,128]{3,2,1,0:T(2,128)S(1)} all-to-all(f32[32,3,2,128]{3,2,1,0:T(2,128)S(1)} %get-tuple-element.74), channel_id=1, replica_groups=mesh['dom'=8,'grp'=4] {'dom','grp'}, dimensions={0} | all-to-all | bytes 196608 | tf_op jit(solution)/shard_map/all_to_all | solution.py:329
  47.7 1.2 apply.9
  48.9 9.5 %all_to_all.89.refs_0_ = f32[32,3,2,128]{3,2,1,0:T(2,128)S(1)} all-to-all(f32[32,3,2,128]{3,2,1,0:T(2,128)S(1)} %get-tuple-element.75), channel_id=1, replica_groups=mesh['dom'=8,'grp'=4] {'dom','grp'}, dimensions={0} | all-to-all | bytes 196608 | tf_op jit(solution)/shard_map/all_to_all | solution.py:329
  58.4 0.2 update.8
  58.6 9.5 %all_to_all.90.recv_ref = f32[32,3,2,128]{3,2,1,0:T(2,128)S(1)} all-to-all(f32[32,3,2,128]{3,2,1,0:T(2,128)S(1)} %get-tuple-element.82), channel_id=1, replica_groups=mesh['dom'=8,'grp'=4] {'dom','grp'}, dimensions={0} | all-to-all | bytes 196608 | tf_op jit(solution)/shard_map/all_to_all | solution.py:329
  68.1 1.3 apply.10
  69.4 9.5 %all_to_all.91.refs_0_ = f32[32,3,2,128]{3,2,1,0:T(2,128)S(1)} all-to-all(f32[32,3,2,128]{3,2,1,0:T(2,128)S(1)} %get-tuple-element.83), channel_id=1, replica_groups=mesh['dom'=8,'grp'=4] {'dom','grp'}, dimensions={0} | all-to-all | bytes 196608 | tf_op jit(solution)/shard_map/all_to_all | solution.py:329
  78.8 0.2 update.9
  79.0 9.5 %all_to_all.92.recv_ref = f32[32,3,2,128]{3,2,1,0:T(2,128)S(1)} all-to-all(f32[32,3,2,128]{3,2,1,0:T(2,128)S(1)} %get-tuple-element.90), channel_id=1, replica_groups=mesh['dom'=8,'grp'=4] {'dom','grp'}, dimensions={0} | all-to-all | bytes 196608 | tf_op jit(solution)/shard_map/all_to_all | solution.py:329
  88.5 1.3 apply.11
  89.8 9.5 %all_to_all.93.refs_0_ = f32[32,3,2,128]{3,2,1,0:T(2,128)S(1)} all-to-all(f32[32,3,2,128]{3,2,1,0:T(2,128)S(1)} %get-tuple-element.91), channel_id=1, replica_groups=mesh['dom'=8,'grp'=4] {'dom','grp'}, dimensions={0} | all-to-all | bytes 196608 | tf_op jit(solution)/shard_map/all_to_all | solution.py:329
  99.3 0.2 update.10
  99.5 9.5 %all_to_all.94.recv_ref = f32[32,3,2,128]{3,2,1,0:T(2,128)S(1)} all-to-all(f32[32,3,2,128]{3,2,1,0:T(2,128)S(1)} %get-tuple-element.98), channel_id=1, replica_groups=mesh['dom'=8,'grp'=4] {'dom','grp'}, dimensions={0} | all-to-all | bytes 196608 | tf_op jit(solution)/shard_map/all_to_all | solution.py:329
  108.9 1.3 apply.12
  110.2 9.5 %all_to_all.95.refs_0_ = f32[32,3,2,128]{3,2,1,0:T(2,128)S(1)} all-to-all(f32[32,3,2,128]{3,2,1,0:T(2,128)S(1)} %get-tuple-element.99), channel_id=1, replica_groups=mesh['dom'=8,'grp'=4] {'dom','grp'}, dimensions={0} | all-to-all | bytes 196608 | tf_op jit(solution)/shard_map/all_to_all | solution.py:329
  119.7 0.2 update.11
  119.9 9.5 %all_to_all.96.recv_ref = f32[32,3,2,128]{3,2,1,0:T(2,128)S(1)} all-to-all(f32[32,3,2,128]{3,2,1,0:T(2,128)S(1)} %get-tuple-element.106), channel_id=1, replica_groups=mesh['dom'=8,'grp'=4] {'dom','grp'}, dimensions={0} | all-to-all | bytes 196608 | tf_op jit(solution)/shard_map/all_to_all | solution.py:329
  129.4 1.3 apply.13
  130.6 9.5 %all_to_all.97.refs_0_ = f32[32,3,2,128]{3,2,1,0:T(2,128)S(1)} all-to-all(f32[32,3,2,128]{3,2,1,0:T(2,128)S(1)} %get-tuple-element.107), channel_id=1, replica_groups=mesh['dom'=8,'grp'=4] {'dom','grp'}, dimensions={0} | all-to-all | bytes 196608 | tf_op jit(solution)/shard_map/all_to_all | solution.py:329
  140.1 0.2 update.12
  140.3 9.5 %all_to_all.98.recv_ref = f32[32,3,2,128]{3,2,1,0:T(2,128)S(1)} all-to-all(f32[32,3,2,128]{3,2,1,0:T(2,128)S(1)} %get-tuple-element.114), channel_id=1, replica_groups=mesh['dom'=8,'grp'=4] {'dom','grp'}, dimensions={0} | all-to-all | bytes 196608 | tf_op jit(solution)/shard_map/all_to_all | solution.py:329
  149.8 1.3 apply.14
  151.0 9.5 %all_to_all.99.refs_0_ = f32[32,3,2,128]{3,2,1,0:T(2,128)S(1)} all-to-all(f32[32,3,2,128]{3,2,1,0:T(2,128)S(1)} %get-tuple-element.115), channel_id=1, replica_groups=mesh['dom'=8,'grp'=4] {'dom','grp'}, dimensions={0} | all-to-all | bytes 196608 | tf_op jit(solution)/shard_map/all_to_all | solution.py:329
  160.5 0.8 update.13
  161.3 9.5 %all_to_all.100.recv_ref = f32[32,3,2,128]{3,2,1,0:T(2,128)S(1)} all-to-all(f32[32,3,2,128]{3,2,1,0:T(2,128)S(1)} %get-tuple-element.122), channel_id=1, replica_groups=mesh['dom'=8,'grp'=4] {'dom','grp'}, dimensions={0} | all-to-all | bytes 196608 | tf_op jit(solution)/shard_map/all_to_all | solution.py:329
  170.8 1.2 apply.15
  172.0 12.3 %all_to_all.101.recv_ref = f32[32,16,128]{2,1,0:T(8,128)S(1)} all-to-all(f32[32,16,128]{2,1,0:T(8,128)S(1)} %get-tuple-element.123), channel_id=1, replica_groups=mesh['dom'=8,'grp'=4] {'dom','grp'}, dimensions={0} | all-to-all | bytes 524288 | tf_op jit(solution)/shard_map/all_to_all | solution.py:329
  184.3 0.7 finish.1

commit v7 on v6

--- a/solution.py
+++ b/solution.py
@@ -260,10 +260,10 @@
     return norm, norm / (cross - beta * norm / scal_ref[1:2, 0:1]), beta
 
 
-def update_kernel(first, width, *refs):
+def update_kernel(first, keep, width, *refs):
     recv_ref, own_ref, r_ref = refs[:3]
-    s_ref, p_ref, x_ref, scal_ref = (None,) * 4 if first else refs[3:7]
-    out_ref, ro_ref, so_ref, po_ref, xo_ref, scalo_ref = refs[-6:]
+    p_ref, x_ref, scal_ref, s_ref = (None,) * 4 if first else refs[3:7]
+    out_ref, po_ref, xo_ref, scalo_ref = refs[-(6 if keep else 4) :][:4]
     faces = own_ref.shape[1]
     plan = Plan(width, faces)
     start = faces - plan.step * (lax.rem(plan.dom, SUB) + 1)
@@ -271,9 +271,11 @@
     shares = []
     for i, w in enumerate(plan.owned(recv_ref)):
         s = w if first else w + beta * s_ref[i]
-        so_ref[i] = s
         shares.append(r_ref[i] - alpha * s)
-        ro_ref[i] = shares[i]
+        if keep:
+            ro_ref, so_ref = refs[-2:]
+            ro_ref[i] = shares[i]
+            so_ref[i] = s
     plan.spread(out_ref, shares)
     own = own_ref[...]
     p = own if first else own + beta * p_ref[...]
@@ -298,7 +300,7 @@
     ro_ref[...] = own - alpha * (w + beta * before)
 
 
-def call(kernel, outs, args, scratch=(), name=None, space=pltpu.VMEM, grant=VMEM_GRANT):
+def call(kernel, outs, args, scratch=(), name=None, space=pltpu.VMEM):
     vmem = pl.BlockSpec(memory_space=pltpu.VMEM)
     return pl.pallas_call(
         kernel,
@@ -307,7 +309,7 @@
         out_specs=jax.tree.map(lambda _: vmem, outs),
         scratch_shapes=list(scratch),
         name=name,
-        compiler_params=pltpu.CompilerParams(vmem_limit_bytes=grant),
+        compiler_params=pltpu.CompilerParams(vmem_limit_bytes=VMEM_GRANT),
     )(*args)
 
 
@@ -357,16 +359,19 @@
         )
         got = exchange(sent)
         if last:
-            _, p, x, scal = state
+            p, x, scal = state
             return call(
                 functools.partial(finish_kernel, width), (field, field), (got, own, past, p, x, scal), name="finish"
             )
-        sent, r, *state = call(
-            functools.partial(update_kernel, first, width),
-            (pieces, shares, shares, field, field, jax.ShapeDtypeStruct((2, faces), f32)),
-            (got, own, r) + tuple(state),
+        keep = iteration + 2 < ITERS
+        sent, *state = call(
+            functools.partial(update_kernel, first, keep, width),
+            (pieces, field, field, jax.ShapeDtypeStruct((2, faces), f32)) + ((shares, shares) if keep else ()),
+            (got, own, r) + tuple(state) + (() if first else (s,)),
             name="update",
         )
+        if keep:
+            *state, r, s = state
         past = own
 
 

time: 185 us -> 185 us (level)
  no operation moved by 1% of the time
where the time goes in v7:
time: 185 us; the launch traced here: 184 us
  blocking collectives  169 us (91%)
  Pallas kernels  14.3 us (8%)
    all_to_all x17, blocking collectives, exchange(): return lax.all_to_all(v, ALL, 0, 0)  169 us
    pallas_call x18, Pallas kernels, call(): pl.pallas_call(kernel, out_shape=outs, in_specs=[pl.BlockSpec(memory_spac...  14.3 us

profile of v7, /device:TPU:0, one launch (start us, length us, event | category | flops | bytes accessed | tf_op | source)
XLA Modules:
  0.0 184.5 jit_solution(17166272467295147339)
XLA Ops:
  0.6 2.2 %rhs.1 = (f32[32,3,2,128]{3,2,1,0:T(2,128)S(1)}, bf16[384,896]{1,0:T(8,128)(2,1)S(1)}, bf16[896,384]{1,0:T(8,128)(2,1)S(1)}, f32[15,128]{1,0:T(8,128)S(1)}, f32[7,15,60,128]{3,2,1,0:T(8,128)S(1)}) custom-call(s32[7,128]{1,0:T(8,128)} %cols_hbm.1, s32[4,128]{1,0:T(4,128)} %owner_hbm.1, bf16[20,80,128]{2,1,0:T(8,128)(2,1)} %inv_hbm.1, ...), custom_call_target="tpu_custom_call" | custom-call | tf_op jit(solution)/shard_map/rhs/pallas_call | solution.py:305
  2.9 14.9 %all_to_all.85.recv_ref = f32[32,3,2,128]{3,2,1,0:T(2,128)S(1)} all-to-all(f32[32,3,2,128]{3,2,1,0:T(2,128)S(1)} %get-tuple-element.65), channel_id=1, replica_groups=mesh['dom'=8,'grp'=4] {'dom','grp'}, dimensions={0} | all-to-all | bytes 196608 | tf_op jit(solution)/shard_map/all_to_all | solution.py:331
  17.8 0.1 start.1
  17.8 9.5 %all_to_all.86.recv_ref = f32[32,3,2,128]{3,2,1,0:T(2,128)S(1)} all-to-all(f32[32,3,2,128]{3,2,1,0:T(2,128)S(1)} %get-tuple-element.66), channel_id=1, replica_groups=mesh['dom'=8,'grp'=4] {'dom','grp'}, dimensions={0} | all-to-all | bytes 196608 | tf_op jit(solution)/shard_map/all_to_all | solution.py:331
  27.3 1.2 apply.8
  28.6 9.5 %all_to_all.87.refs_0_ = f32[32,3,2,128]{3,2,1,0:T(2,128)S(1)} all-to-all(f32[32,3,2,128]{3,2,1,0:T(2,128)S(1)} %get-tuple-element.71), channel_id=1, replica_groups=mesh['dom'=8,'grp'=4] {'dom','grp'}, dimensions={0} | all-to-all | bytes 196608 | tf_op jit(solution)/shard_map/all_to_all | solution.py:331
  38.1 0.1 update.7
  38.2 9.5 %all_to_all.88.recv_ref = f32[32,3,2,128]{3,2,1,0:T(2,128)S(1)} all-to-all(f32[32,3,2,128]{3,2,1,0:T(2,128)S(1)} %get-tuple-element.74), channel_id=1, replica_groups=mesh['dom'=8,'grp'=4] {'dom','grp'}, dimensions={0} | all-to-all | bytes 196608 | tf_op jit(solution)/shard_map/all_to_all | solution.py:331
  47.7 1.2 apply.9
  48.9 9.5 %all_to_all.89.refs_0_ = f32[32,3,2,128]{3,2,1,0:T(2,128)S(1)} all-to-all(f32[32,3,2,128]{3,2,1,0:T(2,128)S(1)} %get-tuple-element.75), channel_id=1, replica_groups=mesh['dom'=8,'grp'=4] {'dom','grp'}, dimensions={0} | all-to-all | bytes 196608 | tf_op jit(solution)/shard_map/all_to_all | solution.py:331
  58.4 0.2 update.8
  58.6 9.5 %all_to_all.90.recv_ref = f32[32,3,2,128]{3,2,1,0:T(2,128)S(1)} all-to-all(f32[32,3,2,128]{3,2,1,0:T(2,128)S(1)} %get-tuple-element.82), channel_id=1, replica_groups=mesh['dom'=8,'grp'=4] {'dom','grp'}, dimensions={0} | all-to-all | bytes 196608 | tf_op jit(solution)/shard_map/all_to_all | solution.py:331
  68.1 1.3 apply.10
  69.4 9.5 %all_to_all.91.refs_0_ = f32[32,3,2,128]{3,2,1,0:T(2,128)S(1)} all-to-all(f32[32,3,2,128]{3,2,1,0:T(2,128)S(1)} %get-tuple-element.83), channel_id=1, replica_groups=mesh['dom'=8,'grp'=4] {'dom','grp'}, dimensions={0} | all-to-all | bytes 196608 | tf_op jit(solution)/shard_map/all_to_all | solution.py:331
  78.8 0.2 update.9
  79.0 9.5 %all_to_all.92.recv_ref = f32[32,3,2,128]{3,2,1,0:T(2,128)S(1)} all-to-all(f32[32,3,2,128]{3,2,1,0:T(2,128)S(1)} %get-tuple-element.90), channel_id=1, replica_groups=mesh['dom'=8,'grp'=4] {'dom','grp'}, dimensions={0} | all-to-all | bytes 196608 | tf_op jit(solution)/shard_map/all_to_all | solution.py:331
  88.5 1.3 apply.11
  89.8 9.5 %all_to_all.93.refs_0_ = f32[32,3,2,128]{3,2,1,0:T(2,128)S(1)} all-to-all(f32[32,3,2,128]{3,2,1,0:T(2,128)S(1)} %get-tuple-element.91), channel_id=1, replica_groups=mesh['dom'=8,'grp'=4] {'dom','grp'}, dimensions={0} | all-to-all | bytes 196608 | tf_op jit(solution)/shard_map/all_to_all | solution.py:331
  99.3 0.2 update.10
  99.5 9.5 %all_to_all.94.recv_ref = f32[32,3,2,128]{3,2,1,0:T(2,128)S(1)} all-to-all(f32[32,3,2,128]{3,2,1,0:T(2,128)S(1)} %get-tuple-element.98), channel_id=1, replica_groups=mesh['dom'=8,'grp'=4] {'dom','grp'}, dimensions={0} | all-to-all | bytes 196608 | tf_op jit(solution)/shard_map/all_to_all | solution.py:331
  108.9 1.3 apply.12
  110.2 9.5 %all_to_all.95.refs_0_ = f32[32,3,2,128]{3,2,1,0:T(2,128)S(1)} all-to-all(f32[32,3,2,128]{3,2,1,0:T(2,128)S(1)} %get-tuple-element.99), channel_id=1, replica_groups=mesh['dom'=8,'grp'=4] {'dom','grp'}, dimensions={0} | all-to-all | bytes 196608 | tf_op jit(solution)/shard_map/all_to_all | solution.py:331
  119.7 0.2 update.11
  119.9 9.5 %all_to_all.96.recv_ref = f32[32,3,2,128]{3,2,1,0:T(2,128)S(1)} all-to-all(f32[32,3,2,128]{3,2,1,0:T(2,128)S(1)} %get-tuple-element.106), channel_id=1, replica_groups=mesh['dom'=8,'grp'=4] {'dom','grp'}, dimensions={0} | all-to-all | bytes 196608 | tf_op jit(solution)/shard_map/all_to_all | solution.py:331
  129.4 1.3 apply.13
  130.6 9.5 %all_to_all.97.refs_0_ = f32[32,3,2,128]{3,2,1,0:T(2,128)S(1)} all-to-all(f32[32,3,2,128]{3,2,1,0:T(2,128)S(1)} %get-tuple-element.107), channel_id=1, replica_groups=mesh['dom'=8,'grp'=4] {'dom','grp'}, dimensions={0} | all-to-all | bytes 196608 | tf_op jit(solution)/shard_map/all_to_all | solution.py:331
  140.1 0.2 update.12
  140.3 9.5 %all_to_all.98.recv_ref = f32[32,3,2,128]{3,2,1,0:T(2,128)S(1)} all-to-all(f32[32,3,2,128]{3,2,1,0:T(2,128)S(1)} %get-tuple-element.114), channel_id=1, replica_groups=mesh['dom'=8,'grp'=4] {'dom','grp'}, dimensions={0} | all-to-all | bytes 196608 | tf_op jit(solution)/shard_map/all_to_all | solution.py:331
  149.8 1.3 apply.14
  151.0 9.5 %all_to_all.99.refs_0_ = f32[32,3,2,128]{3,2,1,0:T(2,128)S(1)} all-to-all(f32[32,3,2,128]{3,2,1,0:T(2,128)S(1)} %get-tuple-element.115), channel_id=1, replica_groups=mesh['dom'=8,'grp'=4] {'dom','grp'}, dimensions={0} | all-to-all | bytes 196608 | tf_op jit(solution)/shard_map/all_to_all | solution.py:331
  160.5 0.2 update.13
  160.7 9.5 %all_to_all.100.recv_ref = f32[32,3,2,128]{3,2,1,0:T(2,128)S(1)} all-to-all(f32[32,3,2,128]{3,2,1,0:T(2,128)S(1)} %get-tuple-element.122), channel_id=1, replica_groups=mesh['dom'=8,'grp'=4] {'dom','grp'}, dimensions={0} | all-to-all | bytes 196608 | tf_op jit(solution)/shard_map/all_to_all | solution.py:331
  170.2 1.2 apply.15
  171.4 12.3 %all_to_all.101.recv_ref = f32[32,16,128]{2,1,0:T(8,128)S(1)} all-to-all(f32[32,16,128]{2,1,0:T(8,128)S(1)} %get-tuple-element.123), channel_id=1, replica_groups=mesh['dom'=8,'grp'=4] {'dom','grp'}, dimensions={0} | all-to-all | bytes 524288 | tf_op jit(solution)/shard_map/all_to_all | solution.py:331
  183.7 0.7 finish.1
